TPU v7x, 128 devices: a whole 4x4x4 slice. The times are simulated.
128 devices in a mesh: patch: 128 (over x, z, y, core).
Axes of the slice: x: 4, y: 4, z: 4, core: 2. Of those that a mesh axis runs over, the one named last changes fastest.
Arguments:
- atm_flux: bfloat16 [8, 393216], P(None, 'patch'), may hold values from -6 to 6
- remap_send: int32 [128, 5, 8], P('patch'), may hold values from 0 to 23
- remap_target: int32 [128, 5, 8], P('patch'), may hold values from 0 to 31
- remap_counts: int32 [128, 5], P('patch'), may hold values from 0 to 8, as said below
- remap_weights: bfloat16 [128, 5, 8, 128, 128], P('patch'), may hold values from -0.5 to 0.5
- coupling: float32 [2, 8], replicated, may hold values from -2 to 2
- tracer: float32 [2, 128, 524288], P(None, None, 'patch'), may hold values from -6 to 6
- wet: int32 [524288], P('patch'), may hold values from 0 to 1
- mix_inverse: float32 [4096, 128, 128], P('patch')
- halo_send: int32 [128, 4, 2, 128], P('patch'), may hold values from 0 to 4095
- halo_ghost: int32 [128, 4, 2, 128], P('patch'), may hold values from 0 to 4095
- halo_rows: int32 [128, 4], P('patch'), may hold values from 0 to 2, as said below
Outputs:
- ocean_flux: float32 [8, 524288], P(None, 'patch')
- tracer_out: float32 [2, 128, 524288], P(None, None, 'patch')
Inputs may be any that keep to these rules, and one draw needn't show every extreme that they name: `remap_counts`: some entry equals 8. `halo_rows`: some entry equals 2.
All inputs are finite; a program needn't handle non-finite values.
Results may differ from a plain program's by a relative error of at most 0.0003.
Values may be sent and summed in bfloat16 or wider, within the bound.
A program may use at most 64 MiB of HBM per device.

v0:
```python
import jax
import jax.numpy as jnp
from jax import lax
from jax.sharding import PartitionSpec as P


def shifted(array, axis, by):
    length = lax.axis_size(axis)
    return lax.ppermute(array, axis, [(i, (i + by) % length) for i in range(length)])


def route_fluxes(outgoing, offsets):
    pieces = [shifted(outgoing[index], "patch", offsets[index]) for index in range(len(offsets))]
    return jnp.stack(pieces)


def route_halo(outgoing, offsets):
    pieces = [shifted(outgoing[index], "patch", offsets[index]) for index in range(len(offsets))]
    return jnp.stack(pieces)


def body(
    atm_flux,
    remap_send,
    remap_target,
    remap_counts,
    remap_weights,
    coupling,
    tracer,
    wet,
    mix_inverse,
    halo_send,
    halo_ghost,
    halo_rows,
):
    offset_count = remap_send.shape[1]
    radius = offset_count // 2
    capacity = remap_send.shape[2]
    block_cells = remap_weights.shape[-1]
    flux_count = atm_flux.shape[0]
    tracers, levels, ocean_cells = tracer.shape
    ocean_blocks = ocean_cells // block_cells
    atm_blocks = atm_flux.shape[1] // block_cells
    wetf = wet.astype(jnp.float32)
    blocks = atm_flux.reshape(flux_count, atm_blocks, block_cells)
    chooser = (
        remap_send[0].reshape(-1)[:, None] == jnp.arange(atm_blocks, dtype=jnp.int32)[None, :]
    ).astype(jnp.bfloat16)
    selected = jnp.einsum(
        "sa,fab->sfb", chooser, blocks, preferred_element_type=jnp.float32
    ).astype(jnp.bfloat16)
    outgoing = selected.reshape(offset_count, capacity, flux_count, block_cells)
    flux_offsets = [index - radius for index in range(offset_count)]
    arrived = route_fluxes(outgoing, flux_offsets)
    in_use = (jnp.arange(capacity, dtype=jnp.int32)[None, :] < remap_counts[0][:, None]).astype(
        jnp.float32
    )
    contrib = jnp.einsum(
        "dcfi,dcij->dcfj", arrived, remap_weights[0], preferred_element_type=jnp.float32
    )
    contrib = contrib * in_use[:, :, None, None]
    table = (remap_target[0][..., None] == jnp.arange(ocean_blocks, dtype=jnp.int32)).astype(
        jnp.float32
    )
    ocean_flux = (
        jnp.einsum("dcb,dcfj->fbj", table, contrib, precision=lax.Precision.HIGHEST).reshape(
            flux_count, ocean_cells
        )
        * wetf
    )
    surface = jnp.dot(coupling, ocean_flux, precision=lax.Precision.HIGHEST)
    rhs = jnp.concatenate([tracer[:, 0:1, :] + surface[:, None, :], tracer[:, 1:, :]], axis=1)
    shaped = rhs.reshape(tracers, levels, ocean_blocks, block_cells)
    solved = jnp.einsum(
        "blk,tkbc->tlbc", mix_inverse, shaped, precision=lax.Precision.HIGHEST
    ).reshape(tracers, levels, ocean_cells)
    mixed = wetf * solved + (1.0 - wetf) * tracer
    sent = mixed.astype(jnp.bfloat16)
    halo_count = halo_send.shape[1]
    halo_depth = halo_send.shape[2]
    lanes = halo_send.shape[3]
    picks = halo_count * halo_depth * lanes
    cell_ids = jnp.arange(ocean_cells, dtype=jnp.int32)
    source_table = (cell_ids[:, None] == halo_send[0].reshape(-1)[None, :]).astype(jnp.bfloat16)
    gathered = jnp.dot(
        sent.reshape(tracers * levels, ocean_cells),
        source_table,
        preferred_element_type=jnp.float32,
    ).astype(jnp.bfloat16)
    gathered = gathered.reshape(tracers, levels, halo_count, halo_depth, lanes)
    halo_offsets = [index - radius for index in range(radius)] + [
        index + 1 for index in range(radius)
    ]
    halo_out = jnp.transpose(gathered, (2, 3, 0, 1, 4))
    received = route_halo(halo_out, halo_offsets)
    values = (
        jnp.transpose(received, (2, 3, 0, 1, 4))
        .reshape(tracers * levels, picks)
        .astype(jnp.float32)
    )
    ghost_table = (halo_ghost[0].reshape(-1)[:, None] == cell_ids[None, :]).astype(jnp.float32)
    flat_mixed = mixed.reshape(tracers * levels, ocean_cells)
    current = lax.dot_general(
        flat_mixed, ghost_table, (((1,), (1,)), ((), ())), precision=lax.Precision.HIGHEST
    )
    ghost_wet = jnp.dot(ghost_table, wetf, precision=lax.Precision.HIGHEST)
    rows_used = (jnp.arange(halo_depth, dtype=jnp.int32)[None, :] < halo_rows[0][:, None]).astype(
        jnp.float32
    )
    weight = (
        jnp.broadcast_to(rows_used[:, :, None], (halo_count, halo_depth, lanes)).reshape(-1)
        * ghost_wet
    )
    increment = 0.25 * (values - current) * weight[None, :]
    added = jnp.dot(increment, ghost_table, precision=lax.Precision.HIGHEST)
    tracer_out = (flat_mixed + added).reshape(tracers, levels, ocean_cells)
    return (ocean_flux, tracer_out)


def solution(mesh):
    return jax.shard_map(
        body,
        mesh=mesh,
        in_specs=(
            P(None, "patch"),
            P("patch", None, None),
            P("patch", None, None),
            P("patch", None),
            P("patch", None, None, None, None),
            P(),
            P(None, None, "patch"),
            P("patch"),
            P("patch", None, None),
            P("patch", None, None, None),
            P("patch", None, None, None),
            P("patch", None),
        ),
        out_specs=(P(None, "patch"), P(None, None, "patch")),
        check_vma=False,
    )
```

profile of v0, /device:TPU:0, one launch (start us, length us, event | category | flops | bytes accessed | tf_op | source)
XLA Modules:
  0.0 118.9 jit_solution(4424167678765149939)
XLA Ops:
  0.6 0.0 copy-start
  0.7 0.8 reduce
  1.5 0.1 eq.60
  1.6 1.0 convolution_convert_fusion
  2.6 8.9 %collective-permute-start = (bf16[8,8,128]{2,0,1:T(8,128)(2,1)S(1)}, bf16[8,8,128]{2,0,1:T(8,128)(2,1)S(1)}, u32[]{:S(2)}, u32[]{:S(2)}) collective-permute-start(bf16[8,8,128]{2,0,1:T(8,128)(2,1)S(1)} %get-tuple-element.12), channel_id=1, source_target_pairs={{0,126},{1,127},{2,0},{3,1},{4,2},{5,3},{6,4},{7,5},{8,6},{9,7},{1... | collective-permute-start | bytes 49160 | tf_op jit(solution)/shard_map/ppermute | solution.py:9
  11.5 0.0 collective-permute-start.1
  11.5 0.0 collective-permute-start.2
  11.5 0.5 collective-permute-start.3
  12.0 0.7 collective-permute-start.4
  12.7 0.7 convert_element_type.41
  13.4 0.7 broadcast_subtract_fusion
  14.1 0.7 fusion.34
  14.8 8.2 %fusion.1 = f32[1,1024]{1,0:T(1,128)S(1)} fusion(f32[4096,1]{0,1:T(1,128)S(1)} %bitcast.96, s32[1024]{0:T(1024)} %bitcast.108), kind=kOutput, calls=%fused_computation.2 | convolution fusion | flops 54525952 | bytes 24576 | tf_op jit(solution)/shard_map/dot_general | solution.py:106
  23.1 0.1 fusion.35
  23.1 1.0 slice.43
  24.1 0.0 copy-start.6
  24.1 5.8 %copy.36 = f32[2,128,4096]{1,2,0:T(8,128)} copy(f32[2,128,4096]{2,1,0:T(8,128)} %param.18) | data formatting | bytes 8388608 | tf_op args[6]
  29.9 0.0 copy-start.7
  29.9 5.4 %slice.54 = f32[2,127,4096]{1,2,0:T(8,128)} slice(f32[2,128,4096]{1,2,0:T(8,128)} %copy.36), slice={[0:2], [1:128], [0:4096]} | slice | bytes 8323072 | tf_op jit(solution)/shard_map/slice | solution.py:72
  35.4 0.4 fusion.22
  35.9 0.3 convolution_bitcast_fusion.1
  36.2 0.1 bitcast_multiply_fusion.1
  36.3 0.0 copy-start.4
  36.3 0.3 fusion.9
  36.6 2.7 %copy.37 = f32[2,1,4096]{1,2,0:T(8,128)} copy(f32[2,1,4096]{2,0,1:T(2,128)S(1)} %fusion.9) | data formatting | bytes 65536 | tf_op jit(solution)/shard_map/add | solution.py:72
  39.3 4.6 %pad_maximum_fusion = f32[2,128,4096]{1,2,0:T(8,128)S(1)} fusion(f32[2,127,4096]{1,2,0:T(8,128)} %slice.54, f32[2,1,4096]{1,2,0:T(8,128)} %copy.37), kind=kLoop, calls=%fused_computation.13 | loop fusion | flops 1048576 | bytes 8388608 | tf_op jit(solution)/shard_map/concatenate | solution.py:72
  43.9 4.5 %fusion.13 = f32[2,128,32,128]{1,3,0,2:T(8,128)S(1)} fusion(f32[2,128,32,128]{1,3,2,0:T(8,128)S(1)} %bitcast.91, f32[32,128,128]{2,1,0:T(8,128)S(1)} %copy-done), kind=kOutput, calls=%fused_computation.18 | convolution fusion | flops 1610612736 | bytes 10485760 | tf_op jit(solution)/shard_map/blk,tkbc->tlbc/dot_general | solution.py:74
  48.4 0.0 copy-start.1
  48.4 0.3 copy.39
  48.7 1.9 %copy-done.1 = f32[2,128,4096]{1,2,0:T(8,128)S(1)} copy-done((f32[2,128,4096]{1,2,0:T(8,128)S(1)}, f32[2,128,4096]{1,2,0:T(8,128)}, u32[]{:S(2)}) %copy-start.1) | copy-done | bytes 4194328
  50.6 4.1 %fusion.36 = (bf16[2,128,4096]{1,2,0:T(8,128)(2,1)}, f32[2,128,4096]{1,2,0:T(8,128)}) fusion(f32[2,128,4096]{1,2,0:T(8,128)S(1)} %copy-done.1, f32[4096]{0:T(1024)S(1)} %broadcast_subtract_fusion, f32[2,128,32,128]{1,3,2,0:T(8,128)S(1)} %copy.39, f32[4096]{0:T(1024)S(1)} %convert_element_type.41), kind=kLoop, calls=%fused_computation.56 | loop fusion | flops 4194304 | bytes 14712832 | tf_op jit(solution)/shard_map/convert_element_type | solution.py:78
  54.7 4.2 %copy.42 = bf16[2,128,4096]{2,1,0:T(8,128)(2,1)} copy(bf16[2,128,4096]{1,2,0:T(8,128)(2,1)} %get-tuple-element.2) | data formatting | bytes 4194304 | tf_op jit(solution)/shard_map/convert_element_type | solution.py:78
  58.9 4.9 %fusion.21 = bf16[256,1024]{1,0:T(8,128)(2,1)S(1)} fusion(bf16[256,4096]{1,0:T(8,128)(2,1)} %bitcast.94, s32[1024]{0:T(1024)S(1)} %bitcast.107), kind=kOutput, calls=%fused_computation.24 | convolution fusion | flops 2151940096 | bytes 2625536 | tf_op jit(solution)/shard_map/dot_general | solution.py:85
  63.8 0.4 reshape.109
  64.2 0.4 copy.66
  64.5 0.4 slice_bitcast_fusion.3
  64.9 6.8 %collective-permute-start.5 = (bf16[2,2,128,128]{3,0,2,1:T(2,128)(2,1)S(1)}, bf16[2,2,128,128]{3,0,2,1:T(2,128)(2,1)S(1)}, u32[]{:S(2)}, u32[]{:S(2)}) collective-permute-start(bf16[2,2,128,128]{3,0,2,1:T(2,128)(2,1)S(1)} %get-tuple-element.4), channel_id=1, source_target_pairs={{0,126},{1,127},{2,0},{3,1},{4,2},{5,3},{6,4},{7,5},{8,6},{9,7},{1... | collective-permute-start | bytes 393224 | tf_op jit(solution)/shard_map/ppermute | solution.py:9
  71.7 0.7 collective-permute-start.6
  72.4 1.2 collective-permute-start.8
  73.6 0.1 broadcast_in_dim.5
  73.7 5.9 %copy.41 = f32[2,128,4096]{2,1,0:T(8,128)} copy(f32[2,128,4096]{1,2,0:T(8,128)} %get-tuple-element.3) | data formatting | bytes 8388608 | tf_op jit(solution)/shard_map/add | solution.py:77
  79.6 3.5 %collective-permute-done.7 = bf16[2,2,128,128]{3,0,2,1:T(2,128)(2,1)S(1)} collective-permute-done((bf16[2,2,128,128]{3,0,2,1:T(2,128)(2,1)S(1)}, bf16[2,2,128,128]{3,0,2,1:T(2,128)(2,1)S(1)}, u32[]{:S(2)}, u32[]{:S(2)}) %collective-permute-start.7) | collective-permute-done | bytes 131104 | tf_op jit(solution)/shard_map/ppermute | solution.py:9
  83.1 1.2 collective-permute-done.8
  84.2 0.7 copy-done.5
  84.9 1.6 %convert_bitcast_fusion = f32[2,128,4,2,128]{4,3,2,1,0:T(2,128)S(1)} fusion(bf16[1,2,2,128,128]{4,1,0,3,2:T(2,128)(2,1)} %bitcast.100, bf16[1,2,2,128,128]{4,1,0,3,2:T(2,128)(2,1)S(1)} %bitcast.99, bf16[1,2,2,128,128]{4,1,0,3,2:T(2,128)(2,1)S(1)} %bitcast.98, bf16[1,2,2,128,128]{4,1,0,3,2:T(2,128)(2,1)S(1)} %bitcast.97), kind=kLoop, calls=%fused_computation.28 | loop fusion | flops 1048576 | bytes 1572864 | tf_op jit(solution)/shard_map/convert_element_type | solution.py:99
  86.5 1.8 %reshape.112 = f32[256,1024]{1,0:T(8,128)} reshape(f32[2,128,4,2,128]{4,3,2,1,0:T(2,128)S(1)} %convert_bitcast_fusion) | data formatting | bytes 2097152 | tf_op jit(solution)/shard_map/convert_element_type | solution.py:99
  88.3 20.4 %fusion.20 = f32[256,1024]{1,0:T(8,128)S(1)} fusion(f32[256,1024]{1,0:T(8,128)} %reshape.112, f32[256,4096]{1,0:T(8,128)} %bitcast.92, s32[1024]{0:T(1024)S(1)} %bitcast.109, f32[1024]{0:T(1024)S(1)} %multiply_multiply_fusion), kind=kOutput, calls=%fused_computation.23 | convolution fusion | flops 12889620480 | bytes 6299648 | tf_op jit(solution)/shard_map/dot_general | solution.py:103
  108.8 10.1 %fusion.8 = f32[256,4096]{1,0:T(8,128)} fusion(f32[256,4096]{1,0:T(8,128)S(1)} %bitcast.93, f32[256,1024]{1,0:T(8,128)S(1)} %fusion.20, s32[1024]{0:T(1024)S(1)} %bitcast.110), kind=kOutput, calls=%fused_computation.10 | convolution fusion | flops 12890144768 | bytes 9441280 | tf_op jit(solution)/shard_map/dot_general | solution.py:115
  (31 shorter events, 0.1 us)
Async XLA Ops:
  0.6 43.3 %copy-start = (f32[32,128,128]{2,1,0:T(8,128)S(1)}, f32[32,128,128]{2,1,0:T(8,128)}, u32[]{:S(2)}) copy-start(f32[32,128,128]{2,1,0:T(8,128)} %param.20) | copy-start | bytes 6291460
  0.6 22.4 %copy-start.8 = (s32[1,4]{1,0:T(1,128)S(1)}, s32[1,4]{1,0:T(1,128)}, u32[]{:S(2)}) copy-start(s32[1,4]{1,0:T(1,128)} %param.23) | copy-start | bytes 52
  2.6 32.7 %collective-permute-start = (bf16[8,8,128]{2,0,1:T(8,128)(2,1)S(1)}, bf16[8,8,128]{2,0,1:T(8,128)(2,1)S(1)}, u32[]{:S(2)}, u32[]{:S(2)}) collective-permute-start(bf16[8,8,128]{2,0,1:T(8,128)(2,1)S(1)} %get-tuple-element.12), channel_id=1, source_target_pairs={{0,126},{1,127},{2,0},{3,1},{4,2},{5,3},{6,4},{7,5},{8,6},{9,7},{1... | collective-permute-start | bytes 49160 | tf_op jit(solution)/shard_map/ppermute | solution.py:9
  11.5 23.8 %collective-permute-start.1 = (bf16[8,8,128]{2,0,1:T(8,128)(2,1)S(1)}, bf16[8,8,128]{2,0,1:T(8,128)(2,1)S(1)}, u32[]{:S(2)}, u32[]{:S(2)}) collective-permute-start(bf16[8,8,128]{2,0,1:T(8,128)(2,1)S(1)} %get-tuple-element.11), channel_id=1, source_target_pairs={{0,127},{1,0},{2,1},{3,2},{4,3},{5,4},{6,5},{7,6},{8,7},{9,8},{10,... | collective-permute-start | bytes 49160 | tf_op jit(solution)/shard_map/ppermute | solution.py:9
  11.5 23.9 %collective-permute-start.2 = (bf16[8,8,128]{2,0,1:T(8,128)(2,1)S(1)}, bf16[8,8,128]{2,0,1:T(8,128)(2,1)S(1)}, u32[]{:S(2)}, u32[]{:S(2)}) collective-permute-start(bf16[8,8,128]{2,0,1:T(8,128)(2,1)S(1)} %get-tuple-element.10), channel_id=1, source_target_pairs={{0,0},{1,1},{2,2},{3,3},{4,4},{5,5},{6,6},{7,7},{8,8},{9,9},{10,10... | collective-permute-start | bytes 49160 | tf_op jit(solution)/shard_map/ppermute | solution.py:9
  11.5 23.9 %collective-permute-start.3 = (bf16[8,8,128]{2,0,1:T(8,128)(2,1)S(1)}, bf16[8,8,128]{2,0,1:T(8,128)(2,1)S(1)}, u32[]{:S(2)}, u32[]{:S(2)}) collective-permute-start(bf16[8,8,128]{2,0,1:T(8,128)(2,1)S(1)} %get-tuple-element.9), channel_id=1, source_target_pairs={{0,1},{1,2},{2,3},{3,4},{4,5},{5,6},{6,7},{7,8},{8,9},{9,10},{10,1... | collective-permute-start | bytes 49160 | tf_op jit(solution)/shard_map/ppermute | solution.py:9
  12.0 23.4 %collective-permute-start.4 = (bf16[8,8,128]{2,0,1:T(8,128)(2,1)S(1)}, bf16[8,8,128]{2,0,1:T(8,128)(2,1)S(1)}, u32[]{:S(2)}, u32[]{:S(2)}) collective-permute-start(bf16[8,8,128]{2,0,1:T(8,128)(2,1)S(1)} %get-tuple-element.8), channel_id=1, source_target_pairs={{0,2},{1,3},{2,4},{3,5},{4,6},{5,7},{6,8},{7,9},{8,10},{9,11},{10,... | collective-permute-start | bytes 49160 | tf_op jit(solution)/shard_map/ppermute | solution.py:9
  24.1 5.8 %copy-start.6 = (s32[1,5,8]{2,0,1:T(1,128)S(1)}, s32[1,5,8]{2,0,1:T(1,128)}, u32[]{:S(2)}) copy-start(s32[1,5,8]{2,0,1:T(1,128)} %param.14) | copy-start | bytes 484
  29.9 5.5 %copy-start.3 = (bf16[1,5,8,128,128]{4,3,2,1,0:T(8,128)(2,1)S(1)}, bf16[1,5,8,128,128]{4,3,2,1,0:T(8,128)(2,1)}, u32[]{:S(2)}) copy-start(bf16[1,5,8,128,128]{4,3,2,1,0:T(8,128)(2,1)} %param.16) | copy-start | bytes 3932164
  29.9 6.4 %copy-start.7 = (f32[2,8]{1,0:T(2,128)S(1)}, f32[2,8]{1,0:T(2,128)}, u32[]{:S(2)}) copy-start(f32[2,8]{1,0:T(2,128)} %param.17) | copy-start | bytes 196
  36.3 7.6 %copy-start.4 = (f32[8,4096]{1,0:T(8,128)}, f32[8,4096]{1,0:T(8,128)S(1)}, u32[]{:S(2)}) copy-start(f32[8,4096]{1,0:T(8,128)S(1)} %bitcast_multiply_fusion.1) | copy-start | bytes 393220
  48.4 2.2 %copy-start.1 = (f32[2,128,4096]{1,2,0:T(8,128)S(1)}, f32[2,128,4096]{1,2,0:T(8,128)}, u32[]{:S(2)}) copy-start(f32[2,128,4096]{1,2,0:T(8,128)} %copy.36) | copy-start | bytes 12582916
  54.7 4.2 %copy-start.9 = (s32[1,4,2,128]{3,2,1,0:T(2,128)S(1)}, s32[1,4,2,128]{3,2,1,0:T(2,128)}, u32[]{:S(2)}) copy-start(s32[1,4,2,128]{3,2,1,0:T(2,128)} %param.21) | copy-start | bytes 12292
  64.9 14.7 %collective-permute-start.5 = (bf16[2,2,128,128]{3,0,2,1:T(2,128)(2,1)S(1)}, bf16[2,2,128,128]{3,0,2,1:T(2,128)(2,1)S(1)}, u32[]{:S(2)}, u32[]{:S(2)}) collective-permute-start(bf16[2,2,128,128]{3,0,2,1:T(2,128)(2,1)S(1)} %get-tuple-element.4), channel_id=1, source_target_pairs={{0,126},{1,127},{2,0},{3,1},{4,2},{5,3},{6,4},{7,5},{8,6},{9,7},{1... | collective-permute-start | bytes 393224 | tf_op jit(solution)/shard_map/ppermute | solution.py:9
  71.7 7.8 %collective-permute-start.6 = (bf16[2,2,128,128]{3,0,2,1:T(2,128)(2,1)S(1)}, bf16[2,2,128,128]{3,0,2,1:T(2,128)(2,1)S(1)}, u32[]{:S(2)}, u32[]{:S(2)}) collective-permute-start(bf16[2,2,128,128]{3,0,2,1:T(2,128)(2,1)S(1)} %get-tuple-element.7), channel_id=1, source_target_pairs={{0,127},{1,0},{2,1},{3,2},{4,3},{5,4},{6,5},{7,6},{8,7},{9,8},{10,... | collective-permute-start | bytes 393224 | tf_op jit(solution)/shard_map/ppermute | solution.py:9
  72.4 10.6 %collective-permute-start.7 = (bf16[2,2,128,128]{3,0,2,1:T(2,128)(2,1)S(1)}, bf16[2,2,128,128]{3,0,2,1:T(2,128)(2,1)S(1)}, u32[]{:S(2)}, u32[]{:S(2)}) collective-permute-start(bf16[2,2,128,128]{3,0,2,1:T(2,128)(2,1)S(1)} %get-tuple-element.6), channel_id=1, source_target_pairs={{0,1},{1,2},{2,3},{3,4},{4,5},{5,6},{6,7},{7,8},{8,9},{9,10},{10,1... | collective-permute-start | bytes 393224 | tf_op jit(solution)/shard_map/ppermute | solution.py:9
  72.4 11.8 %collective-permute-start.8 = (bf16[2,2,128,128]{3,0,2,1:T(2,128)(2,1)S(1)}, bf16[2,2,128,128]{3,0,2,1:T(2,128)(2,1)S(1)}, u32[]{:S(2)}, u32[]{:S(2)}) collective-permute-start(bf16[2,2,128,128]{3,0,2,1:T(2,128)(2,1)S(1)} %get-tuple-element.5), channel_id=1, source_target_pairs={{0,2},{1,3},{2,4},{3,5},{4,6},{5,7},{6,8},{7,9},{8,10},{9,11},{10,... | collective-permute-start | bytes 393224 | tf_op jit(solution)/shard_map/ppermute | solution.py:9
  73.7 14.6 %copy-start.10 = (s32[1,4,2,128]{3,2,1,0:T(2,128)S(1)}, s32[1,4,2,128]{3,2,1,0:T(2,128)}, u32[]{:S(2)}) copy-start(s32[1,4,2,128]{3,2,1,0:T(2,128)} %param.22) | copy-start | bytes 12292
  84.2 0.7 copy-start.5
  88.3 20.4 %copy-start.2 = (f32[2,128,4096]{2,1,0:T(8,128)S(1)}, f32[2,128,4096]{2,1,0:T(8,128)}, u32[]{:S(2)}) copy-start(f32[2,128,4096]{2,1,0:T(8,128)} %copy.41) | copy-start | bytes 12582916
where the time goes:
time: 121 us; the launch traced here: 119 us
  matrix products  50.2 us (41%)
  local copies, waits for them, and re-layouts  30.9 us (26%)
  starting transfers between devices  18.8 us (16%)
  other arithmetic  13.5 us (11%)
  waiting for transfers between devices  4.65 us (4%)
    dot_general x1, matrix products, body(): lax.dot_general(flat_mixed, ghost_table, (((1,), (1,)), ((), ())), precis...  20.4 us
    ppermute x9, starting transfers between devices, shifted(): lax.ppermute(array, axis, [(i, (i + by) % length) for i in range(length)])  18.8 us
    dot_general x1, matrix products, body(): added = jnp.dot(increment, ghost_table, precision=lax.Precision.HIGHEST)  10.1 us
    unnamed x28, local copies, waits for them, and re-layouts  8.42 us
    dot_general x1, matrix products, body(): ghost_wet = jnp.dot(ghost_table, wetf, precision=lax.Precision.HIGHEST)  8.22 us
    add x1, local copies, waits for them, and re-layouts, body(): mixed = wetf * solved + (1.0 - wetf) * tracer  5.9 us
    slice x1, local copies, waits for them, and re-layouts, body(): tracer[:, 1:, :]  5.38 us
    dot_general x1, matrix products, body(): jnp.dot(sent.reshape(tracers * levels, ocean_cells), source_table, prefer...  4.92 us
  transfers between devices with their start and end apart: 9, of which 2 were waited for; matrix products, arithmetic and copies ran while one was open for 24% of the time, Pallas kernels for 0%

commit v1 on v0

v1 whole, which is shorter than its diff:
```python
import functools

import jax
import jax.numpy as jnp
from jax import lax
from jax.experimental import pallas as pl
from jax.experimental.pallas import tpu as pltpu
from jax.sharding import PartitionSpec as P

F = 8
LEV = 128
NTR = 2
BLK = 128
ABLK = 24
OBLK = 32
CAP = 8
SPAN = 5
HSPAN = 4
OC = 4096
CHUNKS = 8
PER = OBLK // CHUNKS
FLUX_OFFSETS = (-2, -1, 0, 1, 2)
HALO_OFFSETS = (-2, -1, 1, 2)
HALO_ORDER = (3, 0, 2, 1)
MESH = pl.DeviceIdType.MESH
f32 = jnp.float32
bf16 = jnp.bfloat16


def split2(v):
    hi = v.astype(bf16)
    lo = (v - hi.astype(f32)).astype(bf16)
    return hi, lo


def split3(v):
    hi, rest = v.astype(bf16), None
    rest = v - hi.astype(f32)
    mid = rest.astype(bf16)
    low = (rest - mid.astype(f32)).astype(bf16)
    return hi, mid, low


def couple(
    size,
    send_s, tgt_s, cnt_s, coup_s, atm_v, hs_v, wet_v, tracer_h, mix_h, w_h,
    mixed_o, v_o, of_o,
    x, m, w, blocks, outg, arr, contrib, ofs, surf, sent, onehot, hout, v,
    xsem, msem, wsem, osem, fs, fr, hsend, hrecv, vsem,
):
    me = lax.axis_index("patch")

    def at(offset):
        return lax.rem(me + (offset + size), size)

    barrier = pltpu.get_barrier_semaphore()
    for offset in HALO_OFFSETS:
        pl.semaphore_signal(barrier, inc=1, device_id=(at(offset),), device_id_type=MESH)

    def xcopy(i):
        cols = pl.ds(pl.multiple_of(i * (PER * BLK), PER * BLK), PER * BLK)
        return pltpu.make_async_copy(tracer_h.at[:, :, cols], x.at[:, :, cols], xsem.at[i])

    def mcopy(i):
        rows = pl.ds(i * PER, PER)
        return pltpu.make_async_copy(mix_h.at[rows], m.at[rows], msem.at[i])

    wcopy = pltpu.make_async_copy(w_h, w, wsem)
    for i in range(CHUNKS):
        xcopy(i).start()
        mcopy(i).start()
    wcopy.start()

    slots = SPAN * CAP
    row40 = lax.broadcasted_iota(jnp.int32, (slots, BLK), 0)
    lane40 = lax.broadcasted_iota(jnp.int32, (slots, BLK), 1)
    want = jnp.full((slots, BLK), -1, jnp.int32)
    for d in range(SPAN):
        for c in range(CAP):
            want = jnp.where(row40 == d * CAP + c, send_s[d, 0, c], want)
    chooser = jnp.where(want == lane40, 1.0, 0.0).astype(bf16)[:, :32]
    for a in range(ABLK):
        blocks[a * F : (a + 1) * F, :] = atm_v[:, a * BLK : (a + 1) * BLK].astype(f32)
    blocks[ABLK * F :, :] = jnp.zeros(((32 - ABLK) * F, BLK), f32)
    for k in range(F // 2):
        pair = jnp.concatenate(
            [blocks[pl.ds(2 * k, 32, stride=F), :], blocks[pl.ds(2 * k + 1, 32, stride=F), :]],
            axis=1,
        )
        chosen = jnp.dot(chooser, pair.astype(bf16), preferred_element_type=f32)
        for q in range(2):
            contrib[pl.ds(2 * k + q, slots, stride=F), :] = chosen[:, q * BLK : (q + 1) * BLK]
    for d in range(SPAN):
        rows = contrib[d * CAP * F : (d + 1) * CAP * F, :].astype(bf16)
        if FLUX_OFFSETS[d] == 0:
            arr[d] = rows
        else:
            outg[d] = rows

    pl.semaphore_wait(barrier, len(HALO_OFFSETS))

    flux = []
    for d in range(SPAN):
        if FLUX_OFFSETS[d] != 0:
            copy = pltpu.make_async_remote_copy(
                src_ref=outg.at[d], dst_ref=arr.at[d], send_sem=fs.at[d], recv_sem=fr.at[d],
                device_id=(at(FLUX_OFFSETS[d]),), device_id_type=MESH,
            )
            copy.start()
            flux.append(copy)

    def solve(i, carry):
        xcopy(i).wait()
        mcopy(i).wait()
        for j in range(PER):
            b = i * PER + j
            cols = pl.ds(pl.multiple_of(b * BLK, BLK), BLK)
            a1, a2 = split2(m[b])
            t = jnp.concatenate([x[0, :, cols], x[1, :, cols]], axis=1)
            b1, b2 = split2(t)
            lhs = jnp.concatenate(
                [jnp.concatenate([a1, a1], axis=1), jnp.concatenate([a2, a2], axis=1)], axis=0
            )
            rhs = jnp.concatenate([b1, b2], axis=0)
            both = jnp.dot(lhs, rhs, preferred_element_type=f32)
            solved = both[:LEV] + both[LEV:]
            row = wet_v[pl.ds(b, 1), :]
            wet = jnp.concatenate([row, row], axis=1) > 0
            base = jnp.where(wet, solved, t)
            x[0, :, cols] = base[:, :BLK]
            x[1, :, cols] = base[:, BLK:]
        return carry

    lax.fori_loop(0, CHUNKS, solve, 0)

    sub = lax.broadcasted_iota(jnp.int32, (BLK, 2 * BLK), 0)
    lows, highs = [], []
    for h in range(HSPAN):
        row = jnp.concatenate([hs_v[2 * h : 2 * h + 1, :], hs_v[2 * h + 1 : 2 * h + 2, :]], axis=1)
        lows.append(jnp.where(sub == (row % BLK), 1.0, 0.0).astype(bf16))
        highs.append(jnp.broadcast_to((row // BLK).astype(f32), (BLK, 2 * BLK)).astype(bf16))
    for h in range(HSPAN):
        def table(b, carry, low=lows[h], high=highs[h], h=h):
            here = high == lax.convert_element_type(b, f32).astype(bf16)
            rows = pl.ds(pl.multiple_of(b * BLK, BLK), BLK)
            onehot[h, rows, :] = jnp.where(here, low, jnp.zeros_like(low))
            return carry

        lax.fori_loop(0, OBLK, table, 0)

    lane = lax.broadcasted_iota(jnp.int32, (OBLK, BLK), 1)
    block = lax.broadcasted_iota(jnp.int32, (OBLK, BLK), 0)
    target = jnp.full((OBLK, BLK), -1, jnp.int32)
    used = jnp.zeros((OBLK, BLK), jnp.int32)
    for d in range(SPAN):
        used = jnp.where(lane // CAP == d, cnt_s[0, d], used)
        for c in range(CAP):
            target = jnp.where(lane == d * CAP + c, tgt_s[d, 0, c], target)
    here = (target == block) & (lane % CAP < used)
    place = jnp.where(here, 1.0, 0.0).astype(bf16)[:, :48]
    contrib[320:384, :] = jnp.zeros((64, BLK), f32)

    wcopy.wait()
    for copy in flux:
        copy.wait_recv()

    slot = lax.broadcasted_iota(jnp.int32, (32, BLK), 0) // F
    for d in range(SPAN):
        for g in range(2):
            c = 4 * g
            pieces = arr[d, c * F : (c + 4) * F, :].astype(f32)
            even = jnp.where(slot % 2 == 0, pieces, 0.0)
            odd = jnp.where(slot % 2 == 1, pieces, 0.0)
            lhs = jnp.concatenate([even, odd], axis=1).astype(bf16)
            rhs = jnp.concatenate(
                [
                    jnp.concatenate([w[d, c], w[d, c + 2]], axis=1),
                    jnp.concatenate([w[d, c + 1], w[d, c + 3]], axis=1),
                ],
                axis=0,
            )
            both = jnp.dot(lhs, rhs, preferred_element_type=f32)
            contrib[(d * CAP + c) * F : (d * CAP + c + 4) * F, :] = jnp.where(
                slot < 2, both[:, :BLK], both[:, BLK:]
            )

    wetf = wet_v[...].astype(f32)
    acc = [jnp.zeros((OBLK, BLK), f32) for _ in range(NTR)]
    for k in range(F // 2):
        pair = jnp.concatenate(
            [contrib[pl.ds(2 * k, 48, stride=F), :], contrib[pl.ds(2 * k + 1, 48, stride=F), :]],
            axis=1,
        )
        c1, c2, c3 = split3(pair)
        total = jnp.dot(place, c1, preferred_element_type=f32)
        total = total + jnp.dot(place, c2, preferred_element_type=f32)
        total = total + jnp.dot(place, c3, preferred_element_type=f32)
        for q in range(2):
            f = 2 * k + q
            flux_f = total[:, q * BLK : (q + 1) * BLK] * wetf
            ofs[pl.ds(f, OBLK, stride=F), :] = flux_f
            for t in range(NTR):
                acc[t] = acc[t] + coup_s[t, f] * flux_f
    for t in range(NTR):
        surf[t] = acc[t]

    def correct(b, carry):
        cols = pl.ds(pl.multiple_of(b * BLK, BLK), BLK)
        first = jnp.broadcast_to(m[b, :, 0:1], (LEV, BLK))
        for t in range(NTR):
            full = x[t, :, cols] + first * surf[t, pl.ds(b, 1), :]
            x[t, :, cols] = full
            sent[t * LEV : (t + 1) * LEV, cols] = full.astype(bf16)
        return carry

    lax.fori_loop(0, OBLK, correct, 0)

    halo = []
    for h in HALO_ORDER:
        picked = jnp.dot(sent[...], onehot[h], preferred_element_type=f32)
        hout[h] = picked.astype(bf16)
        copy = pltpu.make_async_remote_copy(
            src_ref=hout.at[h], dst_ref=v.at[h], send_sem=hsend.at[h], recv_sem=hrecv.at[h],
            device_id=(at(HALO_OFFSETS[h]),), device_id_type=MESH,
        )
        copy.start()
        halo.append(copy)

    done = [pltpu.make_async_copy(x, mixed_o, osem.at[0]), pltpu.make_async_copy(ofs, of_o, osem.at[1])]
    for copy in done:
        copy.start()
    for h, copy in zip(HALO_ORDER, halo):
        copy.wait_recv()
        out = pltpu.make_async_copy(v.at[h], v_o.at[h], vsem.at[h])
        out.start()
        done.append(out)
    for copy in flux:
        copy.wait_send()
    for copy in halo:
        copy.wait_send()
    for copy in done:
        copy.wait()


COLS = 512


def scatter(rows_s, ghost_v, wet_v, v_v, mixed_v, of_v, flux_o, out_o, table):
    blocks = COLS // BLK
    base = pl.program_id(0) * blocks
    sub = lax.broadcasted_iota(jnp.int32, (BLK, BLK), 0)
    for p in range(2 * HSPAN):
        row = ghost_v[p : p + 1, :]
        used = (p % 2) < rows_s[0, p // 2]
        row = jnp.where(used, row, -1)
        low = jnp.where(sub == (row & (BLK - 1)), 1.0, 0.0)
        high = jnp.broadcast_to(row >> 7, (BLK, BLK))
        for j in range(blocks):
            table[j * BLK : (j + 1) * BLK, p * BLK : (p + 1) * BLK] = jnp.where(
                high == base + j, low, 0.0
            ).astype(bf16)
    ones = jnp.ones((16, 2 * BLK * HSPAN), bf16)
    values = jnp.concatenate([v_v[h] for h in range(HSPAN)], axis=1)
    lhs = jnp.concatenate([values, ones], axis=0)
    total = lax.dot_general(
        lhs, table[...], (((1,), (1,)), ((), ())), preferred_element_type=f32
    )
    rows = pl.ds(pl.multiple_of(base, blocks), blocks)
    quarter = 0.25 * wet_v[rows, :].astype(f32)
    weight = jnp.concatenate([quarter[j : j + 1, :] for j in range(blocks)], axis=1)
    count = total[NTR * LEV : NTR * LEV + 1, :]
    for t in range(NTR):
        mixed = mixed_v[t]
        out_o[t] = mixed + weight * (total[t * LEV : (t + 1) * LEV] - count * mixed)
    for j in range(blocks):
        flux_o[:, j * BLK : (j + 1) * BLK] = of_v[j * F : (j + 1) * F, :]


def body(
    atm_flux, remap_send, remap_target, remap_counts, remap_weights, coupling,
    tracer, wet, mix_inverse, halo_send, halo_ghost, halo_rows,
):
    size = lax.axis_size("patch")
    wet2 = wet.reshape(OBLK, BLK)
    sends = halo_send.reshape(2 * HSPAN, BLK)
    ghosts = halo_ghost.reshape(2 * HSPAN, BLK)
    weights = remap_weights.reshape(SPAN, CAP, BLK, BLK)
    smem = pl.BlockSpec(memory_space=pltpu.SMEM)
    vmem = pl.BlockSpec(memory_space=pltpu.VMEM)
    hbm = pl.BlockSpec(memory_space=pltpu.HBM)
    dma = pltpu.SemaphoreType.DMA
    mixed, values, flux = pl.pallas_call(
        functools.partial(couple, size),
        name="couple",
        out_shape=(
            jax.ShapeDtypeStruct((NTR, LEV, OC), f32),
            jax.ShapeDtypeStruct((HSPAN, NTR * LEV, 2 * BLK), bf16),
            jax.ShapeDtypeStruct((OBLK * F, BLK), f32),
        ),
        in_specs=[smem] * 4 + [vmem] * 3 + [hbm] * 3,
        out_specs=(hbm, hbm, hbm),
        scratch_shapes=[
            pltpu.VMEM((NTR, LEV, OC), f32),
            pltpu.VMEM((OBLK, LEV, LEV), f32),
            pltpu.VMEM((SPAN, CAP, BLK, BLK), bf16),
            pltpu.VMEM((32 * F, BLK), f32),
            pltpu.VMEM((SPAN, CAP * F, BLK), bf16),
            pltpu.VMEM((SPAN, CAP * F, BLK), bf16),
            pltpu.VMEM((48 * F, BLK), f32),
            pltpu.VMEM((OBLK * F, BLK), f32),
            pltpu.VMEM((NTR, OBLK, BLK), f32),
            pltpu.VMEM((NTR * LEV, OC), bf16),
            pltpu.VMEM((HSPAN, OC, 2 * BLK), bf16),
            pltpu.VMEM((HSPAN, NTR * LEV, 2 * BLK), bf16),
            pltpu.VMEM((HSPAN, NTR * LEV, 2 * BLK), bf16),
            dma((CHUNKS,)), dma((CHUNKS,)), dma(()), dma((2,)),
            dma((SPAN,)), dma((SPAN,)), dma((HSPAN,)), dma((HSPAN,)), dma((HSPAN,)),
        ],
        compiler_params=pltpu.CompilerParams(
            collective_id=0, has_side_effects=True, vmem_limit_bytes=67043328
        ),
    )(
        jnp.transpose(remap_send, (1, 0, 2)), jnp.transpose(remap_target, (1, 0, 2)),
        remap_counts, coupling, atm_flux, sends, wet2,
        tracer, mix_inverse, weights,
    )
    whole = lambda shape: pl.BlockSpec(shape, lambda i: (0,) * len(shape))
    return pl.pallas_call(
        scatter,
        name="scatter",
        grid=(OC // COLS,),
        out_shape=(
            jax.ShapeDtypeStruct((F, OC), f32),
            jax.ShapeDtypeStruct((NTR, LEV, OC), f32),
        ),
        in_specs=[
            smem,
            whole((2 * HSPAN, BLK)),
            whole((OBLK, BLK)),
            whole((HSPAN, NTR * LEV, 2 * BLK)),
            pl.BlockSpec((NTR, LEV, COLS), lambda i: (0, 0, i)),
            pl.BlockSpec((COLS // BLK * F, BLK), lambda i: (i, 0)),
        ],
        out_specs=(
            pl.BlockSpec((F, COLS), lambda i: (0, i)),
            pl.BlockSpec((NTR, LEV, COLS), lambda i: (0, 0, i)),
        ),
        scratch_shapes=[pltpu.VMEM((COLS, 2 * BLK * HSPAN), bf16)],
        compiler_params=pltpu.CompilerParams(vmem_limit_bytes=67043328),
    )(halo_rows, ghosts, wet2, values, mixed, flux)


def solution(mesh):
    return jax.shard_map(
        body,
        mesh=mesh,
        in_specs=(
            P(None, "patch"),
            P("patch", None, None),
            P("patch", None, None),
            P("patch", None),
            P("patch", None, None, None, None),
            P(),
            P(None, None, "patch"),
            P("patch"),
            P("patch", None, None),
            P("patch", None, None, None),
            P("patch", None, None, None),
            P("patch", None),
        ),
        out_specs=(P(None, "patch"), P(None, None, "patch")),
        check_vma=False,
    )
```

time: 121 us -> 41.4 us (0.34); the launches traced: 119 us -> 41 us
  matrix products: 50.2 us -> 0 us
  Pallas kernels: 0 us -> 40.4 us
  local copies, waits for them, and re-layouts: 30.9 us -> 0 us
  starting transfers between devices: 18.8 us -> 0 us
  other arithmetic: 13.5 us -> 0 us
  waiting for transfers between devices: 4.65 us -> 0 us
    dot_general x9 -> x0, matrix products: 50.2 us -> none  [the longest x1 20.4 us: body(): lax.dot_general(flat_mixed, ghost_table, (((1,), (1,)), ((), ())), precis...]
    pallas_call x0 -> x2, Pallas kernels: none -> 40.4 us  [the longest x1 30.9 us: body(): pl.pallas_call(functools.partial(couple, size), name='couple', out_shape=...]
    ppermute x9 -> x0, starting transfers between devices: 18.8 us -> none  [shifted(): lax.ppermute(array, axis, [(i, (i + by) % length) for i in range(length)])]
    add x2 -> x0, local copies, waits for them, and re-layouts: 8.6 us -> none  [the longest x1 5.9 us: body(): mixed = wetf * solved + (1.0 - wetf) * tracer]
    unnamed x28 -> x0, local copies, waits for them, and re-layouts: 8.42 us -> none
    convert_element_type x5 -> x0, other arithmetic: 7.23 us -> none  [the longest x1 4.1 us: body(): sent = mixed.astype(jnp.bfloat16)]
    slice x3 -> x0, local copies, waits for them, and re-layouts: 6.38 us -> none  [the longest x1 5.38 us: body(): tracer[:, 1:, :]]
    convert_element_type x2 -> x0, local copies, waits for them, and re-layouts: 5.96 us -> none  [the longest x1 4.15 us: body(): sent = mixed.astype(jnp.bfloat16)]
  transfers between devices with their start and end apart: 9 -> 0, of which waited for: 2 -> 0; matrix products, arithmetic and copies ran while one was open for 24% -> 0% of each run, Pallas kernels for 0% -> 0%
where the time goes in v1:
time: 41.4 us; the launch traced here: 41 us
  Pallas kernels  40.4 us (98%)
  between operations  0.64 us (2%)
    pallas_call x1, Pallas kernels, body(): pl.pallas_call(functools.partial(couple, size), name='couple', out_shape=...  30.9 us
    pallas_call x1, Pallas kernels, body(): pl.pallas_call(scatter, name='scatter', grid=(OC // COLS,), out_shape=(ja...  9.52 us

profile of v1, /device:TPU:0, one launch (start us, length us, event | category | flops | bytes accessed | tf_op | source)
XLA Modules:
  0.0 41.0 jit_solution(6012709041662029913)
XLA Ops:
  0.6 30.9 %couple.1 = (f32[2,128,4096]{2,1,0:T(8,128)}, bf16[4,256,256]{2,1,0:T(8,128)(2,1)}, f32[256,128]{1,0:T(8,128)}) custom-call(s32[5,1,8]{2,1,0:T(1,128)} %bitcast.11, s32[5,1,8]{2,1,0:T(1,128)} %bitcast.12, s32[1,5]{1,0:T(1,128)} %cnt_s.1, f32[2,8]{1,0:T(2,128)} %coup_s.1, bf16[8,3072]{1,0:T(8,128)(2,1)} %atm_v.1, s32[8,128]{1,0:T(8,128)} %bitcast.9, ...), custom_call_target="tpu_custom_call" | custom-call | tf_op jit(solution)/shard_map/couple/pallas_call | solution.py:292
  31.5 9.5 %scatter.1 = (f32[8,4096]{1,0:T(8,128)}, f32[2,128,4096]{2,1,0:T(8,128)}) custom-call(s32[1,4]{1,0:T(1,128)} %rows_s.1, s32[8,128]{1,0:T(8,128)} %bitcast.10, s32[32,128]{1,0:T(8,128)} %bitcast.8, bf16[4,256,256]{2,1,0:T(8,128)(2,1)} %get-tuple-element.5.v_v, f32[2,128,4096]{2,1,0:T(8,128)} %get-tuple-element.6.mixed_v, f32[256,128]{1,0:T(8,128)} %get-tuple-element.7.of_v), custom_call_target="tpu_custom_call" | custom-call | tf_op jit(solution)/shard_map/scatter/pallas_call | solution.py:328

commit v2 on v1

v2 whole, which is shorter than its diff:
```python
import functools

import jax
import jax.numpy as jnp
from jax import lax
from jax.experimental import pallas as pl
from jax.experimental.pallas import tpu as pltpu
from jax.sharding import PartitionSpec as P

F = 8
LEV = 128
NTR = 2
BLK = 128
ABLK = 24
OBLK = 32
CAP = 8
SPAN = 5
HSPAN = 4
OC = 4096
PER = 4
FLUX_OFFSETS = (-2, -1, 0, 1, 2)
HALO_OFFSETS = (-2, -1, 1, 2)
HALO_ORDER = (3, 0, 2, 1)
MESH = pl.DeviceIdType.MESH
f32 = jnp.float32
bf16 = jnp.bfloat16


def split2(v):
    hi = v.astype(bf16)
    lo = (v - hi.astype(f32)).astype(bf16)
    return hi, lo


def split3(v):
    hi, rest = v.astype(bf16), None
    rest = v - hi.astype(f32)
    mid = rest.astype(bf16)
    low = (rest - mid.astype(f32)).astype(bf16)
    return hi, mid, low


def couple(
    size,
    send_s, tgt_s, cnt_s, coup_s, rows_s, atm_v, hs_v, hg_v, wet_v, tracer_h, mix_h, w_h,
    x, ofs, last_v, last_low, last_high, quarter_o,
    m, w, blocks, outg, arr, contrib, surf, scale, sent, low_t, high_t, hout, v,
    xsem, msem, wsem, fs, fr, hsend, hrecv,
):
    me = lax.axis_index("patch")

    def at(offset):
        return lax.rem(me + (offset + size), size)

    barrier = pltpu.get_barrier_semaphore()
    for offset in HALO_OFFSETS:
        pl.semaphore_signal(barrier, inc=1, device_id=(at(offset),), device_id_type=MESH)

    def xcopy(b, t):
        cols = pl.ds(pl.multiple_of(b * BLK, BLK), BLK)
        return pltpu.make_async_copy(tracer_h.at[t, :, cols], x.at[b, t], xsem.at[b, t])

    def mcopy(i):
        rows = pl.ds(i * PER, PER)
        return pltpu.make_async_copy(mix_h.at[rows], m.at[rows], msem.at[i])

    wcopy = pltpu.make_async_copy(w_h, w, wsem)
    for i in range(OBLK // PER):
        mcopy(i).start()
        for b in range(i * PER, (i + 1) * PER):
            for t in range(NTR):
                xcopy(b, t).start()
    wcopy.start()

    slots = SPAN * CAP
    row40 = lax.broadcasted_iota(jnp.int32, (slots, BLK), 0)
    lane40 = lax.broadcasted_iota(jnp.int32, (slots, BLK), 1)
    want = jnp.full((slots, BLK), -1, jnp.int32)
    for d in range(SPAN):
        for c in range(CAP):
            want = jnp.where(row40 == d * CAP + c, send_s[d, 0, c], want)
    chooser = jnp.where(want == lane40, 1.0, 0.0).astype(bf16)[:, :32]
    for a in range(ABLK):
        blocks[a * F : (a + 1) * F, :] = atm_v[:, a * BLK : (a + 1) * BLK].astype(f32)
    blocks[ABLK * F :, :] = jnp.zeros(((32 - ABLK) * F, BLK), f32)
    for k in range(F // 2):
        pair = jnp.concatenate(
            [blocks[pl.ds(2 * k, 32, stride=F), :], blocks[pl.ds(2 * k + 1, 32, stride=F), :]],
            axis=1,
        )
        chosen = jnp.dot(chooser, pair.astype(bf16), preferred_element_type=f32)
        for q in range(2):
            contrib[pl.ds(2 * k + q, slots, stride=F), :] = chosen[:, q * BLK : (q + 1) * BLK]
    for d in range(SPAN):
        rows = contrib[d * CAP * F : (d + 1) * CAP * F, :].astype(bf16)
        if FLUX_OFFSETS[d] == 0:
            arr[d] = rows
        else:
            outg[d] = rows

    pl.semaphore_wait(barrier, len(HALO_OFFSETS))

    flux = []
    for d in range(SPAN):
        if FLUX_OFFSETS[d] != 0:
            copy = pltpu.make_async_remote_copy(
                src_ref=outg.at[d], dst_ref=arr.at[d], send_sem=fs.at[d], recv_sem=fr.at[d],
                device_id=(at(FLUX_OFFSETS[d]),), device_id_type=MESH,
            )
            copy.start()
            flux.append(copy)

    def solve(i, carry):
        mcopy(i).wait()
        for j in range(PER):
            b = i * PER + j
            for t in range(NTR):
                xcopy(b, t).wait()
            a1, a2 = split2(m[b])
            t = jnp.concatenate([x[b, 0], x[b, 1]], axis=1)
            b1, b2 = split2(t)
            lhs = jnp.concatenate(
                [jnp.concatenate([a1, a1], axis=1), jnp.concatenate([a2, a2], axis=1)], axis=0
            )
            rhs = jnp.concatenate([b1, b2], axis=0)
            both = jnp.dot(lhs, rhs, preferred_element_type=f32)
            solved = both[:LEV] + both[LEV:]
            row = wet_v[pl.ds(b, 1), :]
            wet = jnp.concatenate([row, row], axis=1) > 0
            base = jnp.where(wet, solved, t)
            x[b, 0] = base[:, :BLK]
            x[b, 1] = base[:, BLK:]
        return carry

    lax.fori_loop(0, OBLK // PER, solve, 0)

    lane128 = lax.broadcasted_iota(jnp.int32, (BLK, BLK), 1).astype(f32)
    block32 = lax.broadcasted_iota(jnp.int32, (OBLK, BLK), 0)
    count = jnp.zeros((OBLK, BLK), f32)
    for h in range(HSPAN):
        for r in range(2):
            ghost = hg_v[2 * h + r : 2 * h + r + 1, :]
            spread = jnp.broadcast_to(ghost & (BLK - 1), (BLK, BLK)).astype(f32)
            low = jnp.where(jnp.transpose(spread) == lane128, 1.0, 0.0).astype(bf16)
            high = jnp.where(r < rows_s[0, h], ghost >> 7, -1)
            low_t[h, r * BLK : (r + 1) * BLK, :] = low
            spread = jnp.broadcast_to(high, (BLK, BLK)).astype(f32)
            high_t[h, r * BLK : (r + 1) * BLK, :] = jnp.transpose(spread).astype(bf16)
            here = jnp.where(block32 == high, 1.0, 0.0).astype(bf16)
            count = count + jnp.dot(here, low, preferred_element_type=f32)
    quarter = 0.25 * wet_v[...].astype(f32)
    quarter_o[...] = quarter
    scale[...] = 1.0 - quarter * count
    last = HALO_ORDER[-1]
    last_low[...] = low_t[last]
    last_high[...] = high_t[last]

    sub = lax.broadcasted_iota(jnp.int32, (BLK, 2 * BLK), 0)

    def send_table(h):
        row = jnp.concatenate([hs_v[2 * h : 2 * h + 1, :], hs_v[2 * h + 1 : 2 * h + 2, :]], axis=1)
        low = jnp.where(sub == (row & (BLK - 1)), 1.0, 0.0).astype(bf16)
        high = jnp.broadcast_to((row >> 7).astype(f32), (BLK, 2 * BLK)).astype(bf16)
        return low, high

    lane = lax.broadcasted_iota(jnp.int32, (OBLK, BLK), 1)
    target = jnp.full((OBLK, BLK), -1, jnp.int32)
    used = jnp.zeros((OBLK, BLK), jnp.int32)
    for d in range(SPAN):
        used = jnp.where(lane // CAP == d, cnt_s[0, d], used)
        for c in range(CAP):
            target = jnp.where(lane == d * CAP + c, tgt_s[d, 0, c], target)
    here = (target == block32) & (lane % CAP < used)
    place = jnp.where(here, 1.0, 0.0).astype(bf16)[:, :48]
    contrib[320:384, :] = jnp.zeros((64, BLK), f32)

    wcopy.wait()
    for copy in flux:
        copy.wait_recv()

    slot = lax.broadcasted_iota(jnp.int32, (32, BLK), 0) // F
    for d in range(SPAN):
        for g in range(2):
            c = 4 * g
            pieces = arr[d, c * F : (c + 4) * F, :].astype(f32)
            even = jnp.where(slot % 2 == 0, pieces, 0.0)
            odd = jnp.where(slot % 2 == 1, pieces, 0.0)
            lhs = jnp.concatenate([even, odd], axis=1).astype(bf16)
            rhs = jnp.concatenate(
                [
                    jnp.concatenate([w[d, c], w[d, c + 2]], axis=1),
                    jnp.concatenate([w[d, c + 1], w[d, c + 3]], axis=1),
                ],
                axis=0,
            )
            both = jnp.dot(lhs, rhs, preferred_element_type=f32)
            contrib[(d * CAP + c) * F : (d * CAP + c + 4) * F, :] = jnp.where(
                slot < 2, both[:, :BLK], both[:, BLK:]
            )

    wetf = wet_v[...].astype(f32)
    acc = [jnp.zeros((OBLK, BLK), f32) for _ in range(NTR)]
    for k in range(F // 2):
        pair = jnp.concatenate(
            [contrib[pl.ds(2 * k, 48, stride=F), :], contrib[pl.ds(2 * k + 1, 48, stride=F), :]],
            axis=1,
        )
        c1, c2, c3 = split3(pair)
        total = jnp.dot(place, c1, preferred_element_type=f32)
        total = total + jnp.dot(place, c2, preferred_element_type=f32)
        total = total + jnp.dot(place, c3, preferred_element_type=f32)
        for q in range(2):
            f = 2 * k + q
            flux_f = total[:, q * BLK : (q + 1) * BLK] * wetf
            ofs[pl.ds(f, OBLK, stride=F), :] = flux_f
            for t in range(NTR):
                acc[t] = acc[t] + coup_s[t, f] * flux_f
    for t in range(NTR):
        surf[t] = acc[t]

    halo = []
    for n, h in enumerate(HALO_ORDER):
        low, high = send_table(h)
        picked = jnp.zeros((NTR * LEV, 2 * BLK), f32)
        for k in range(OBLK // 2):
            tables, tiles = [], []
            for b in (2 * k, 2 * k + 1):
                tables.append(jnp.where(high == jnp.array(b, bf16), low, jnp.zeros_like(low)))
                if n == 0:
                    first = jnp.broadcast_to(m[b, :, 0:1], (LEV, BLK))
                    tiles.append(
                        jnp.concatenate(
                            [x[b, t] + first * surf[t, b : b + 1, :] for t in range(NTR)], axis=0
                        ).astype(bf16)
                    )
            if n == 0:
                tile = jnp.concatenate(tiles, axis=1)
                sent[k] = tile
            else:
                tile = sent[k]
            picked = picked + jnp.dot(
                tile, jnp.concatenate(tables, axis=0), preferred_element_type=f32
            )
        hout[h] = picked.astype(bf16)
        copy = pltpu.make_async_remote_copy(
            src_ref=hout.at[h], dst_ref=v.at[h], send_sem=hsend.at[h], recv_sem=hrecv.at[h],
            device_id=(at(HALO_OFFSETS[h]),), device_id_type=MESH,
        )
        copy.start()
        halo.append(copy)

    def finish(b, carry):
        first = jnp.broadcast_to(m[b, :, 0:1], (LEV, BLK))
        keep = scale[pl.ds(b, 1), :]
        for t in range(NTR):
            x[b, t] = (x[b, t] + first * surf[t, pl.ds(b, 1), :]) * keep
        return carry

    lax.fori_loop(0, OBLK, finish, 0)

    for h, copy in zip(HALO_ORDER, halo):
        copy.wait_recv()
        if h == last:
            last_v[...] = v[h]
        else:
            def spread_values(k, carry, h=h):
                add_values(k, x, v[h], low_t[h], high_t[h], quarter_o, x)
                return carry

            lax.fori_loop(0, OBLK // 2, spread_values, 0)
    for copy in flux:
        copy.wait_send()
    for copy in halo:
        copy.wait_send()


def add_values(k, x, values, low, high, quarter_v, out):
    tables = []
    for j in range(2):
        b = lax.convert_element_type(2 * k + j, f32).astype(bf16)
        tables.append(jnp.where(high == b, low, jnp.zeros_like(low)))
    total = jnp.dot(values, jnp.concatenate(tables, axis=1), preferred_element_type=f32)
    for j in range(2):
        b = 2 * k + j
        weight = quarter_v[pl.ds(b, 1), :]
        for t in range(NTR):
            part = total[t * LEV : (t + 1) * LEV, j * BLK : (j + 1) * BLK]
            out[b, t] = x[b, t] + weight * part


def scatter(x, ofs, values_v, low_v, high_v, quarter_v, flux_o, out_o, stage, line, sem, fsem):
    for b in range(OBLK):
        line[:, b * BLK : (b + 1) * BLK] = ofs[b * F : (b + 1) * F, :]
    fcopy = pltpu.make_async_copy(line, flux_o, fsem)
    fcopy.start()

    def ocopy(b, t):
        cols = pl.ds(pl.multiple_of(b * BLK, BLK), BLK)
        return pltpu.make_async_copy(stage.at[b, t], out_o.at[t, :, cols], sem.at[b, t])

    def step(k, carry):
        add_values(k, x, values_v[...], low_v[...], high_v[...], quarter_v, stage)
        for j in range(2):
            for t in range(NTR):
                ocopy(2 * k + j, t).start()
        return carry

    lax.fori_loop(0, OBLK // 2, step, 0)

    def drain(b, carry):
        for t in range(NTR):
            ocopy(b, t).wait()
        return carry

    lax.fori_loop(0, OBLK, drain, 0)
    fcopy.wait()


def body(
    atm_flux, remap_send, remap_target, remap_counts, remap_weights, coupling,
    tracer, wet, mix_inverse, halo_send, halo_ghost, halo_rows,
):
    size = lax.axis_size("patch")
    wet2 = wet.reshape(OBLK, BLK)
    sends = halo_send.reshape(2 * HSPAN, BLK)
    ghosts = halo_ghost.reshape(2 * HSPAN, BLK)
    weights = remap_weights.reshape(SPAN, CAP, BLK, BLK)
    far = lambda a: pltpu.with_memory_space_constraint(a, pltpu.HBM)
    smem = pl.BlockSpec(memory_space=pltpu.SMEM)
    vmem = pl.BlockSpec(memory_space=pltpu.VMEM)
    hbm = pl.BlockSpec(memory_space=pltpu.HBM)
    dma = pltpu.SemaphoreType.DMA
    picks = 2 * BLK
    between = pl.pallas_call(
        functools.partial(couple, size),
        name="couple",
        out_shape=(
            jax.ShapeDtypeStruct((OBLK, NTR, LEV, BLK), f32),
            jax.ShapeDtypeStruct((OBLK * F, BLK), f32),
            jax.ShapeDtypeStruct((NTR * LEV, picks), bf16),
            jax.ShapeDtypeStruct((picks, BLK), bf16),
            jax.ShapeDtypeStruct((picks, BLK), bf16),
            jax.ShapeDtypeStruct((OBLK, BLK), f32),
        ),
        in_specs=[smem] * 5 + [vmem] * 4 + [hbm] * 3,
        out_specs=(vmem,) * 6,
        scratch_shapes=[
            pltpu.VMEM((OBLK, LEV, LEV), f32),
            pltpu.VMEM((SPAN, CAP, BLK, BLK), bf16),
            pltpu.VMEM((32 * F, BLK), f32),
            pltpu.VMEM((SPAN, CAP * F, BLK), bf16),
            pltpu.VMEM((SPAN, CAP * F, BLK), bf16),
            pltpu.VMEM((48 * F, BLK), f32),
            pltpu.VMEM((NTR, OBLK, BLK), f32),
            pltpu.VMEM((OBLK, BLK), f32),
            pltpu.VMEM((OBLK // 2, NTR * LEV, 2 * BLK), bf16),
            pltpu.VMEM((HSPAN, picks, BLK), bf16),
            pltpu.VMEM((HSPAN, picks, BLK), bf16),
            pltpu.VMEM((HSPAN, NTR * LEV, picks), bf16),
            pltpu.VMEM((HSPAN, NTR * LEV, picks), bf16),
            dma((OBLK, NTR)), dma((OBLK // PER,)), dma(()),
            dma((SPAN,)), dma((SPAN,)), dma((HSPAN,)), dma((HSPAN,)),
        ],
        compiler_params=pltpu.CompilerParams(
            collective_id=0, has_side_effects=True, vmem_limit_bytes=24 * 1024 * 1024
        ),
    )(
        far(jnp.transpose(remap_send, (1, 0, 2))), far(jnp.transpose(remap_target, (1, 0, 2))),
        far(remap_counts), far(coupling), far(halo_rows), far(atm_flux), far(sends), far(ghosts),
        far(wet2), far(tracer), far(mix_inverse), far(weights),
    )
    return pl.pallas_call(
        scatter,
        name="scatter",
        out_shape=(
            jax.ShapeDtypeStruct((F, OC), f32),
            jax.ShapeDtypeStruct((NTR, LEV, OC), f32),
        ),
        in_specs=[vmem] * 6,
        out_specs=(hbm, hbm),
        scratch_shapes=[
            pltpu.VMEM((OBLK, NTR, LEV, BLK), f32),
            pltpu.VMEM((F, OC), f32),
            dma((OBLK, NTR)), dma(()),
        ],
        compiler_params=pltpu.CompilerParams(vmem_limit_bytes=16 * 1024 * 1024),
    )(*between)


def solution(mesh):
    return jax.shard_map(
        body,
        mesh=mesh,
        in_specs=(
            P(None, "patch"),
            P("patch", None, None),
            P("patch", None, None),
            P("patch", None),
            P("patch", None, None, None, None),
            P(),
            P(None, None, "patch"),
            P("patch"),
            P("patch", None, None),
            P("patch", None, None, None),
            P("patch", None, None, None),
            P("patch", None),
        ),
        out_specs=(P(None, "patch"), P(None, None, "patch")),
        check_vma=False,
    )
```

time: 41.4 us -> 41.8 us (level)
    pallas_call x1, Pallas kernels: 30.9 us -> 36.1 us  [body(): pl.pallas_call(functools.partial(couple, size), name='couple', out_shape=...]
    pallas_call x1, Pallas kernels: 9.52 us -> 4.52 us  [body(): pl.pallas_call(scatter, name='scatter', out_shape=(jax.ShapeDtypeStruct((...]
where the time goes in v2:
time: 41.8 us; the launch traced here: 41.2 us
  Pallas kernels  40.6 us (97%)
  between operations  0.64 us (2%)
    pallas_call x1, Pallas kernels, body(): pl.pallas_call(functools.partial(couple, size), name='couple', out_shape=...  36.1 us
    pallas_call x1, Pallas kernels, body(): pl.pallas_call(scatter, name='scatter', out_shape=(jax.ShapeDtypeStruct((...  4.52 us

profile of v2, /device:TPU:0, one launch (start us, length us, event | category | flops | bytes accessed | tf_op | source)
XLA Modules:
  0.0 41.2 jit_solution(15307790520969683342)
XLA Ops:
  0.6 36.1 %couple.1 = (f32[32,2,128,128]{3,2,1,0:T(8,128)S(1)}, f32[256,128]{1,0:T(8,128)S(1)}, bf16[256,256]{1,0:T(8,128)(2,1)S(1)}, bf16[256,128]{1,0:T(8,128)(2,1)S(1)}...) custom-call(s32[5,1,8]{2,1,0:T(1,128)} %bitcast.10, s32[5,1,8]{2,1,0:T(1,128)} %bitcast.11, s32[1,5]{1,0:T(1,128)} %cnt_s.1, ...), custom_call_target="tpu_custom_call" | custom-call | tf_op jit(solution)/shard_map/couple/pallas_call | solution.py:334
  36.7 4.5 %scatter.1 = (f32[8,4096]{1,0:T(8,128)}, f32[2,128,4096]{2,1,0:T(8,128)}) custom-call(f32[32,2,128,128]{3,2,1,0:T(8,128)S(1)} %get-tuple-element.8.x, f32[256,128]{1,0:T(8,128)S(1)} %get-tuple-element.9.ofs, bf16[256,256]{1,0:T(8,128)(2,1)S(1)} %get-tuple-element.10.values_v, bf16[256,128]{1,0:T(8,128)(2,1)S(1)} %get-tuple-element.11.low_v, ...), custom_call_target="tpu_custom_call" | custom-call | tf_op jit(solution)/shard_map/scatter/pallas_call | solution.py:372

commit v3 on v2

--- a/solution.py
+++ b/solution.py
@@ -17,7 +17,7 @@
 SPAN = 5
 HSPAN = 4
 OC = 4096
-PER = 4
+PER = 8
 FLUX_OFFSETS = (-2, -1, 0, 1, 2)
 HALO_OFFSETS = (-2, -1, 1, 2)
 HALO_ORDER = (3, 0, 2, 1)
@@ -110,29 +110,26 @@
             copy.start()
             flux.append(copy)
 
-    def solve(i, carry):
-        mcopy(i).wait()
-        for j in range(PER):
-            b = i * PER + j
-            for t in range(NTR):
-                xcopy(b, t).wait()
-            a1, a2 = split2(m[b])
-            t = jnp.concatenate([x[b, 0], x[b, 1]], axis=1)
-            b1, b2 = split2(t)
-            lhs = jnp.concatenate(
-                [jnp.concatenate([a1, a1], axis=1), jnp.concatenate([a2, a2], axis=1)], axis=0
-            )
-            rhs = jnp.concatenate([b1, b2], axis=0)
-            both = jnp.dot(lhs, rhs, preferred_element_type=f32)
-            solved = both[:LEV] + both[LEV:]
-            row = wet_v[pl.ds(b, 1), :]
-            wet = jnp.concatenate([row, row], axis=1) > 0
-            base = jnp.where(wet, solved, t)
-            x[b, 0] = base[:, :BLK]
-            x[b, 1] = base[:, BLK:]
-        return carry
-
-    lax.fori_loop(0, OBLK // PER, solve, 0)
+    for b in range(OBLK):
+        if b % PER == 0:
+            mcopy(b // PER).wait()
+            for n in range(PER):
+                for t in range(NTR):
+                    xcopy(b + n, t).wait()
+        a1, a2 = split2(m[b])
+        t = jnp.concatenate([x[b, 0], x[b, 1]], axis=1)
+        b1, b2 = split2(t)
+        lhs = jnp.concatenate(
+            [jnp.concatenate([a1, a1], axis=1), jnp.concatenate([a2, a2], axis=1)], axis=0
+        )
+        rhs = jnp.concatenate([b1, b2], axis=0)
+        both = jnp.dot(lhs, rhs, preferred_element_type=f32)
+        solved = both[:LEV] + both[LEV:]
+        row = wet_v[b : b + 1, :]
+        wet = jnp.concatenate([row, row], axis=1) > 0
+        base = jnp.where(wet, solved, t)
+        x[b, 0] = base[:, :BLK]
+        x[b, 1] = base[:, BLK:]
 
     lane128 = lax.broadcasted_iota(jnp.int32, (BLK, BLK), 1).astype(f32)
     block32 = lax.broadcasted_iota(jnp.int32, (OBLK, BLK), 0)
@@ -228,11 +225,10 @@
                 tables.append(jnp.where(high == jnp.array(b, bf16), low, jnp.zeros_like(low)))
                 if n == 0:
                     first = jnp.broadcast_to(m[b, :, 0:1], (LEV, BLK))
-                    tiles.append(
-                        jnp.concatenate(
-                            [x[b, t] + first * surf[t, b : b + 1, :] for t in range(NTR)], axis=0
-                        ).astype(bf16)
-                    )
+                    mixed = [x[b, t] + first * surf[t, b : b + 1, :] for t in range(NTR)]
+                    for t in range(NTR):
+                        x[b, t] = mixed[t] * scale[b : b + 1, :]
+                    tiles.append(jnp.concatenate(mixed, axis=0).astype(bf16))
             if n == 0:
                 tile = jnp.concatenate(tiles, axis=1)
                 sent[k] = tile
@@ -249,25 +245,13 @@
         copy.start()
         halo.append(copy)
 
-    def finish(b, carry):
-        first = jnp.broadcast_to(m[b, :, 0:1], (LEV, BLK))
-        keep = scale[pl.ds(b, 1), :]
-        for t in range(NTR):
-            x[b, t] = (x[b, t] + first * surf[t, pl.ds(b, 1), :]) * keep
-        return carry
-
-    lax.fori_loop(0, OBLK, finish, 0)
-
     for h, copy in zip(HALO_ORDER, halo):
         copy.wait_recv()
         if h == last:
             last_v[...] = v[h]
         else:
-            def spread_values(k, carry, h=h):
+            for k in range(OBLK // 2):
                 add_values(k, x, v[h], low_t[h], high_t[h], quarter_o, x)
-                return carry
-
-            lax.fori_loop(0, OBLK // 2, spread_values, 0)
     for copy in flux:
         copy.wait_send()
     for copy in halo:
@@ -277,12 +261,12 @@
 def add_values(k, x, values, low, high, quarter_v, out):
     tables = []
     for j in range(2):
-        b = lax.convert_element_type(2 * k + j, f32).astype(bf16)
-        tables.append(jnp.where(high == b, low, jnp.zeros_like(low)))
+        here = high == jnp.array(2 * k + j, bf16)
+        tables.append(jnp.where(here, low, jnp.zeros_like(low)))
     total = jnp.dot(values, jnp.concatenate(tables, axis=1), preferred_element_type=f32)
     for j in range(2):
         b = 2 * k + j
-        weight = quarter_v[pl.ds(b, 1), :]
+        weight = quarter_v[b : b + 1, :]
         for t in range(NTR):
             part = total[t * LEV : (t + 1) * LEV, j * BLK : (j + 1) * BLK]
             out[b, t] = x[b, t] + weight * part
@@ -298,14 +282,11 @@
         cols = pl.ds(pl.multiple_of(b * BLK, BLK), BLK)
         return pltpu.make_async_copy(stage.at[b, t], out_o.at[t, :, cols], sem.at[b, t])
 
-    def step(k, carry):
+    for k in range(OBLK // 2):
         add_values(k, x, values_v[...], low_v[...], high_v[...], quarter_v, stage)
         for j in range(2):
             for t in range(NTR):
                 ocopy(2 * k + j, t).start()
-        return carry
-
-    lax.fori_loop(0, OBLK // 2, step, 0)
 
     def drain(b, carry):
         for t in range(NTR):

time: 41.8 us -> 31.9 us (0.76)
  Pallas kernels: 40.6 us -> 31 us
    pallas_call x1, Pallas kernels: 36.1 us -> 28.2 us  [body(): pl.pallas_call(functools.partial(couple, size), name='couple', out_shape=...]
    pallas_call x1, Pallas kernels: 4.52 us -> 2.84 us  [body(): pl.pallas_call(scatter, name='scatter', out_shape=(jax.ShapeDtypeStruct((...]
where the time goes in v3:
time: 31.9 us; the launch traced here: 31.7 us
  Pallas kernels  31 us (97%)
  between operations  0.64 us (2%)
    pallas_call x1, Pallas kernels, body(): pl.pallas_call(functools.partial(couple, size), name='couple', out_shape=...  28.2 us
    pallas_call x1, Pallas kernels, body(): pl.pallas_call(scatter, name='scatter', out_shape=(jax.ShapeDtypeStruct((...  2.84 us

profile of v3, /device:TPU:0, one launch (start us, length us, event | category | flops | bytes accessed | tf_op | source)
XLA Modules:
  0.0 31.7 jit_solution(2970829287209113531)
XLA Ops:
  0.6 28.2 %couple.1 = (f32[32,2,128,128]{3,2,1,0:T(8,128)S(1)}, f32[256,128]{1,0:T(8,128)S(1)}, bf16[256,256]{1,0:T(8,128)(2,1)S(1)}, bf16[256,128]{1,0:T(8,128)(2,1)S(1)}...) custom-call(s32[5,1,8]{2,1,0:T(1,128)} %bitcast.10, s32[5,1,8]{2,1,0:T(1,128)} %bitcast.11, s32[1,5]{1,0:T(1,128)} %cnt_s.1, ...), custom_call_target="tpu_custom_call" | custom-call | tf_op jit(solution)/shard_map/couple/pallas_call | solution.py:315
  28.8 2.8 %scatter.1 = (f32[8,4096]{1,0:T(8,128)}, f32[2,128,4096]{2,1,0:T(8,128)}) custom-call(f32[32,2,128,128]{3,2,1,0:T(8,128)S(1)} %get-tuple-element.8.x, f32[256,128]{1,0:T(8,128)S(1)} %get-tuple-element.9.ofs, bf16[256,256]{1,0:T(8,128)(2,1)S(1)} %get-tuple-element.10.values_v, bf16[256,128]{1,0:T(8,128)(2,1)S(1)} %get-tuple-element.11.low_v, ...), custom_call_target="tpu_custom_call" | custom-call | tf_op jit(solution)/shard_map/scatter/pallas_call | solution.py:353

commit v4 on v3

v4 whole, which is shorter than its diff:
```python
import functools

import jax
import jax.numpy as jnp
from jax import lax
from jax.experimental import pallas as pl
from jax.experimental.pallas import tpu as pltpu
from jax.sharding import PartitionSpec as P

F = 8
LEV = 128
NTR = 2
BLK = 128
ABLK = 24
OBLK = 32
CAP = 8
SPAN = 5
HSPAN = 4
OC = 4096
PER = 8
FLUX_OFFSETS = (-2, -1, 0, 1, 2)
HALO_OFFSETS = (-2, -1, 1, 2)
SEND_ORDERS = ((3, 0, 2, 1), (0, 1, 3, 2), (3, 0, 2, 1), (3, 2, 0, 1))
WAIT_ORDERS = (((3, 2, 1, 0), (3, 2, 0, 1)), ((0, 1, 3, 2), (0, 1, 2, 3)))
LINE = 4
MESH = pl.DeviceIdType.MESH
f32 = jnp.float32
bf16 = jnp.bfloat16


def split2(v):
    hi = v.astype(bf16)
    lo = (v - hi.astype(f32)).astype(bf16)
    return hi, lo


def split3(v):
    hi, rest = v.astype(bf16), None
    rest = v - hi.astype(f32)
    mid = rest.astype(bf16)
    low = (rest - mid.astype(f32)).astype(bf16)
    return hi, mid, low


def couple(
    size,
    send_h, tgt_h, cnt_h, coup_h, rows_h, atm_h, hs_h, hg_h, wet_h, tracer_h, mix_h, w_h,
    x, line, last_v, last_low, last_high, quarter_o,
    send_s, tgt_s, cnt_s, coup_s, rows_s, atm_v, hs_v, hg_v, wet_v,
    m, w, blocks, outg, arr, contrib, ofs, surf, scale, sent, low_t, high_t, hout, v,
    small, xsem, msem, wsem, fs, fr, hsend, hrecv,
):
    me = lax.axis_index("patch")

    def at(offset):
        return lax.rem(me + (offset + size), size)

    barrier = pltpu.get_barrier_semaphore()
    for offset in HALO_OFFSETS:
        pl.semaphore_signal(barrier, inc=1, device_id=(at(offset),), device_id_type=MESH)

    chip = lax.rem(me // 2, LINE)
    top = (chip + 1) // LINE
    foot = (LINE - chip) // LINE
    upper = chip // (LINE // 2)
    core = lax.rem(me, 2)

    def choose(i):
        high, low = WAIT_ORDERS
        above = high[0][i] * (1 - core) + high[1][i] * core
        below = low[0][i] * (1 - core) + low[1][i] * core
        return above * upper + below * (1 - upper)

    order = [choose(i) for i in range(HSPAN)]
    second = (1 - foot) * (1 - upper)
    third = (1 - top) * upper
    places = (foot, second, third, top)
    sends = [sum(SEND_ORDERS[y][i] * places[y] for y in range(LINE)) for i in range(HSPAN)]

    pairs = (
        (send_h, send_s), (atm_h, atm_v), (wet_h, wet_v), (hs_h, hs_v), (hg_h, hg_v),
        (tgt_h, tgt_s), (cnt_h, cnt_s), (coup_h, coup_s), (rows_h, rows_s),
    )
    smalls = [pltpu.make_async_copy(src, dst, small.at[i]) for i, (src, dst) in enumerate(pairs)]
    for copy in smalls:
        copy.start()

    def xcopy(b, t):
        cols = pl.ds(pl.multiple_of(b * BLK, BLK), BLK)
        return pltpu.make_async_copy(tracer_h.at[t, :, cols], x.at[b, t], xsem.at[b // PER])

    def mcopy(i):
        rows = pl.ds(i * PER, PER)
        return pltpu.make_async_copy(mix_h.at[rows], m.at[rows], msem.at[i])

    wcopy = pltpu.make_async_copy(w_h, w, wsem)

    def fetch(i):
        mcopy(i).start()
        for b in range(i * PER, (i + 1) * PER):
            for t in range(NTR):
                xcopy(b, t).start()

    for copy in smalls[:3]:
        copy.wait()
    fetch(0)
    fetch(1)
    slots = SPAN * CAP
    row40 = lax.broadcasted_iota(jnp.int32, (slots, BLK), 0)
    lane40 = lax.broadcasted_iota(jnp.int32, (slots, BLK), 1)
    want = jnp.full((slots, BLK), -1, jnp.int32)
    for d in range(SPAN):
        for c in range(CAP):
            want = jnp.where(row40 == d * CAP + c, send_s[d, 0, c], want)
    chooser = jnp.where(want == lane40, 1.0, 0.0).astype(bf16)[:, :32]
    for a in range(ABLK):
        blocks[a * F : (a + 1) * F, :] = atm_v[:, a * BLK : (a + 1) * BLK].astype(f32)
    blocks[ABLK * F :, :] = jnp.zeros(((32 - ABLK) * F, BLK), f32)
    for k in range(F // 2):
        pair = jnp.concatenate(
            [blocks[pl.ds(2 * k, 32, stride=F), :], blocks[pl.ds(2 * k + 1, 32, stride=F), :]],
            axis=1,
        )
        chosen = jnp.dot(chooser, pair.astype(bf16), preferred_element_type=f32)
        for q in range(2):
            contrib[pl.ds(2 * k + q, slots, stride=F), :] = chosen[:, q * BLK : (q + 1) * BLK]
    for d in range(SPAN):
        rows = contrib[d * CAP * F : (d + 1) * CAP * F, :].astype(bf16)
        if FLUX_OFFSETS[d] == 0:
            arr[d] = rows
        else:
            outg[d] = rows

    for i in range(2, OBLK // PER):
        fetch(i)
    wcopy.start()

    def solve(i):
        mcopy(i).wait()
        chunk = x.at[pl.ds(i * PER, PER)]
        pltpu.make_async_copy(chunk, chunk, xsem.at[i]).wait()
        for b in range(i * PER, (i + 1) * PER):
            a1, a2 = split2(m[b])
            t = jnp.concatenate([x[b, 0], x[b, 1]], axis=1)
            b1, b2 = split2(t)
            lhs = jnp.concatenate(
                [jnp.concatenate([a1, a1], axis=1), jnp.concatenate([a2, a2], axis=1)], axis=0
            )
            rhs = jnp.concatenate([b1, b2], axis=0)
            both = jnp.dot(lhs, rhs, preferred_element_type=f32)
            solved = both[:LEV] + both[LEV:]
            row = wet_v[b : b + 1, :]
            wet = jnp.concatenate([row, row], axis=1) > 0
            base = jnp.where(wet, solved, t)
            x[b, 0] = base[:, :BLK]
            x[b, 1] = base[:, BLK:]

    pl.semaphore_wait(barrier, len(HALO_OFFSETS))

    flux = []
    for d in range(SPAN):
        if FLUX_OFFSETS[d] != 0:
            copy = pltpu.make_async_remote_copy(
                src_ref=outg.at[d], dst_ref=arr.at[d], send_sem=fs.at[d], recv_sem=fr.at[d],
                device_id=(at(FLUX_OFFSETS[d]),), device_id_type=MESH,
            )
            copy.start()
            flux.append(copy)

    for i in range(OBLK // PER):
        solve(i)
    for copy in smalls[3:]:
        copy.wait()

    lane128 = lax.broadcasted_iota(jnp.int32, (BLK, BLK), 1).astype(f32)
    block32 = lax.broadcasted_iota(jnp.int32, (OBLK, BLK), 0)
    count = jnp.zeros((OBLK, BLK), f32)
    for h in range(HSPAN):
        for r in range(2):
            ghost = hg_v[2 * h + r : 2 * h + r + 1, :]
            spread = jnp.broadcast_to(ghost & (BLK - 1), (BLK, BLK)).astype(f32)
            low = jnp.where(jnp.transpose(spread) == lane128, 1.0, 0.0).astype(bf16)
            high = jnp.where(r < rows_s[0, h], ghost >> 7, -1)
            low_t[h, r * BLK : (r + 1) * BLK, :] = low
            spread = jnp.broadcast_to(high, (BLK, BLK)).astype(f32)
            high_t[h, r * BLK : (r + 1) * BLK, :] = jnp.transpose(spread).astype(bf16)
            here = jnp.where(block32 == high, 1.0, 0.0).astype(bf16)
            count = count + jnp.dot(here, low, preferred_element_type=f32)
    quarter = 0.25 * wet_v[...].astype(f32)
    quarter_o[...] = quarter
    scale[...] = 1.0 - quarter * count

    lane = lax.broadcasted_iota(jnp.int32, (OBLK, BLK), 1)
    target = jnp.full((OBLK, BLK), -1, jnp.int32)
    used = jnp.zeros((OBLK, BLK), jnp.int32)
    for d in range(SPAN):
        used = jnp.where(lane // CAP == d, cnt_s[0, d], used)
        for c in range(CAP):
            target = jnp.where(lane == d * CAP + c, tgt_s[d, 0, c], target)
    here = (target == block32) & (lane % CAP < used)
    place = jnp.where(here, 1.0, 0.0).astype(bf16)[:, :48]
    contrib[320:384, :] = jnp.zeros((64, BLK), f32)

    wcopy.wait()
    slot = lax.broadcasted_iota(jnp.int32, (32, BLK), 0) // F
    for i in range(SPAN):
        d = i + top * (SPAN - 1 - 2 * i)
        if i != SPAN // 2:
            pltpu.make_async_remote_copy(
                src_ref=outg.at[d], dst_ref=arr.at[d], send_sem=fs.at[d], recv_sem=fr.at[d],
                device_id=(at(1),), device_id_type=MESH,
            ).wait_recv()
        for g in range(2):
            c = 4 * g
            pieces = arr[d, c * F : (c + 4) * F, :].astype(f32)
            even = jnp.where(slot % 2 == 0, pieces, 0.0)
            odd = jnp.where(slot % 2 == 1, pieces, 0.0)
            lhs = jnp.concatenate([even, odd], axis=1).astype(bf16)
            rhs = jnp.concatenate(
                [
                    jnp.concatenate([w[d, c], w[d, c + 2]], axis=1),
                    jnp.concatenate([w[d, c + 1], w[d, c + 3]], axis=1),
                ],
                axis=0,
            )
            both = jnp.dot(lhs, rhs, preferred_element_type=f32)
            rows = pl.ds(pl.multiple_of((d * CAP + c) * F, 4 * F), 4 * F)
            contrib[rows, :] = jnp.where(slot < 2, both[:, :BLK], both[:, BLK:])

    wetf = wet_v[...].astype(f32)
    acc = [jnp.zeros((OBLK, BLK), f32) for _ in range(NTR)]
    for k in range(F // 2):
        pair = jnp.concatenate(
            [contrib[pl.ds(2 * k, 48, stride=F), :], contrib[pl.ds(2 * k + 1, 48, stride=F), :]],
            axis=1,
        )
        c1, c2, c3 = split3(pair)
        total = jnp.dot(place, c1, preferred_element_type=f32)
        total = total + jnp.dot(place, c2, preferred_element_type=f32)
        total = total + jnp.dot(place, c3, preferred_element_type=f32)
        for q in range(2):
            f = 2 * k + q
            flux_f = total[:, q * BLK : (q + 1) * BLK] * wetf
            ofs[pl.ds(f, OBLK, stride=F), :] = flux_f
            for t in range(NTR):
                acc[t] = acc[t] + coup_s[t, f] * flux_f
    for t in range(NTR):
        surf[t] = acc[t]

    sub = lax.broadcasted_iota(jnp.int32, (BLK, 2 * BLK), 0)

    def halo_copy(h, t):
        offset = h - 2 + h // 2
        return pltpu.make_async_remote_copy(
            src_ref=hout.at[h, t], dst_ref=v.at[h, t],
            send_sem=hsend.at[h, t], recv_sem=hrecv.at[h, t],
            device_id=(at(offset),), device_id_type=MESH,
        )

    for n, h in enumerate(sends):
        row = jnp.concatenate([hs_v[pl.ds(2 * h, 1), :], hs_v[pl.ds(2 * h + 1, 1), :]], axis=1)
        low = jnp.where(sub == (row & (BLK - 1)), 1.0, 0.0).astype(bf16)
        high = jnp.broadcast_to((row >> 7).astype(f32), (BLK, 2 * BLK)).astype(bf16)
        for part in ((0,), (1,)) if n == 0 else ((0, 1),):
            rows = slice(part[0] * LEV, (part[-1] + 1) * LEV)
            picked = jnp.zeros((len(part) * LEV, 2 * BLK), f32)
            for k in range(OBLK // 2):
                tables, tiles = [], []
                for b in (2 * k, 2 * k + 1):
                    tables.append(jnp.where(high == jnp.array(b, bf16), low, jnp.zeros_like(low)))
                    if n == 0:
                        first = jnp.broadcast_to(m[b, :, 0:1], (LEV, BLK))
                        for t in part:
                            mixed = x[b, t] + first * surf[t, b : b + 1, :]
                            x[b, t] = mixed * scale[b : b + 1, :]
                            tiles.append(mixed.astype(bf16))
                if n == 0:
                    tile = jnp.concatenate(tiles, axis=1)
                    sent[k, rows] = tile
                else:
                    tile = sent[k, rows]
                picked = picked + jnp.dot(
                    tile, jnp.concatenate(tables, axis=0), preferred_element_type=f32
                )
            for j, t in enumerate(part):
                hout[h, t] = picked[j * LEV : (j + 1) * LEV].astype(bf16)
                halo_copy(h, t).start()

    for b in range(OBLK):
        line[:, b * BLK : (b + 1) * BLK] = ofs[b * F : (b + 1) * F, :]
    last = order[-1]
    last_low[...] = low_t[last]
    last_high[...] = high_t[last]

    for h in order[:-1]:
        for t in range(NTR):
            halo_copy(h, t).wait_recv()
        values = jnp.concatenate([v[h, 0], v[h, 1]], axis=0)
        add_values(x, values, low_t[h], high_t[h], quarter_o)
    for t in range(NTR):
        halo_copy(last, t).wait_recv()
        last_v[t * LEV : (t + 1) * LEV] = v[last, t]
    for copy in flux:
        copy.wait_send()
    for h in order:
        for t in range(NTR):
            halo_copy(h, t).wait_send()


def add_values(x, values, low, high, quarter_v, out=None, ready=None):
    out = x if out is None else out
    for k in range(OBLK // 2):
        tables = []
        for b in (2 * k, 2 * k + 1):
            here = high == jnp.array(b, bf16)
            tables.append(jnp.where(here, low, jnp.zeros_like(low)))
        total = jnp.dot(values, jnp.concatenate(tables, axis=1), preferred_element_type=f32)
        for j, b in enumerate((2 * k, 2 * k + 1)):
            weight = quarter_v[b : b + 1, :]
            for t in range(NTR):
                piece = total[t * LEV : (t + 1) * LEV, j * BLK : (j + 1) * BLK]
                out[b, t] = x[b, t] + weight * piece
                if ready is not None:
                    ready(b, t)


def scatter(x, line, values_v, low_v, high_v, quarter_v, flux_o, out_o, stage, sem, fsem):
    fcopy = pltpu.make_async_copy(line, flux_o, fsem)
    fcopy.start()

    def ready(b, t):
        cols = slice(b * BLK, (b + 1) * BLK)
        pltpu.make_async_copy(stage.at[b, t], out_o.at[t, :, cols], sem).start()

    add_values(x, values_v[...], low_v[...], high_v[...], quarter_v, stage, ready)
    pltpu.make_async_copy(out_o, out_o, sem).wait()
    fcopy.wait()


def body(
    atm_flux, remap_send, remap_target, remap_counts, remap_weights, coupling,
    tracer, wet, mix_inverse, halo_send, halo_ghost, halo_rows,
):
    size = lax.axis_size("patch")
    far = lambda a: pltpu.with_memory_space_constraint(a, pltpu.HBM)
    vmem = pl.BlockSpec(memory_space=pltpu.VMEM)
    hbm = pl.BlockSpec(memory_space=pltpu.HBM)
    dma = pltpu.SemaphoreType.DMA
    i32 = jnp.int32
    picks = 2 * BLK
    between = pl.pallas_call(
        functools.partial(couple, size),
        name="couple",
        out_shape=(
            jax.ShapeDtypeStruct((OBLK, NTR, LEV, BLK), f32),
            jax.ShapeDtypeStruct((F, OC), f32),
            jax.ShapeDtypeStruct((NTR * LEV, picks), bf16),
            jax.ShapeDtypeStruct((picks, BLK), bf16),
            jax.ShapeDtypeStruct((picks, BLK), bf16),
            jax.ShapeDtypeStruct((OBLK, BLK), f32),
        ),
        in_specs=[hbm] * 12,
        out_specs=(vmem,) * 6,
        scratch_shapes=[
            pltpu.SMEM((SPAN, 1, CAP), i32),
            pltpu.SMEM((SPAN, 1, CAP), i32),
            pltpu.SMEM((1, SPAN), i32),
            pltpu.SMEM((NTR, F), f32),
            pltpu.SMEM((1, HSPAN), i32),
            pltpu.VMEM((F, ABLK * BLK), bf16),
            pltpu.VMEM((2 * HSPAN, BLK), i32),
            pltpu.VMEM((2 * HSPAN, BLK), i32),
            pltpu.VMEM((OBLK, BLK), i32),
            pltpu.VMEM((OBLK, LEV, LEV), f32),
            pltpu.VMEM((SPAN, CAP, BLK, BLK), bf16),
            pltpu.VMEM((32 * F, BLK), f32),
            pltpu.VMEM((SPAN, CAP * F, BLK), bf16),
            pltpu.VMEM((SPAN, CAP * F, BLK), bf16),
            pltpu.VMEM((48 * F, BLK), f32),
            pltpu.VMEM((OBLK * F, BLK), f32),
            pltpu.VMEM((NTR, OBLK, BLK), f32),
            pltpu.VMEM((OBLK, BLK), f32),
            pltpu.VMEM((OBLK // 2, NTR * LEV, 2 * BLK), bf16),
            pltpu.VMEM((HSPAN, picks, BLK), bf16),
            pltpu.VMEM((HSPAN, picks, BLK), bf16),
            pltpu.VMEM((HSPAN, NTR, LEV, picks), bf16),
            pltpu.VMEM((HSPAN, NTR, LEV, picks), bf16),
            dma((9,)), dma((OBLK // PER,)), dma((OBLK // PER,)), dma(()),
            dma((SPAN,)), dma((SPAN,)), dma((HSPAN, NTR)), dma((HSPAN, NTR)),
        ],
        compiler_params=pltpu.CompilerParams(
            collective_id=0, has_side_effects=True, vmem_limit_bytes=24 * 1024 * 1024
        ),
    )(
        far(jnp.transpose(remap_send, (1, 0, 2))), far(jnp.transpose(remap_target, (1, 0, 2))),
        far(remap_counts), far(coupling), far(halo_rows), far(atm_flux),
        far(halo_send.reshape(2 * HSPAN, BLK)), far(halo_ghost.reshape(2 * HSPAN, BLK)),
        far(wet.reshape(OBLK, BLK)), far(tracer), far(mix_inverse),
        far(remap_weights.reshape(SPAN, CAP, BLK, BLK)),
    )
    return pl.pallas_call(
        scatter,
        name="scatter",
        out_shape=(
            jax.ShapeDtypeStruct((F, OC), f32),
            jax.ShapeDtypeStruct((NTR, LEV, OC), f32),
        ),
        in_specs=[vmem] * 6,
        out_specs=(hbm, hbm),
        scratch_shapes=[pltpu.VMEM((OBLK, NTR, LEV, BLK), f32), dma(()), dma(())],
        compiler_params=pltpu.CompilerParams(vmem_limit_bytes=16 * 1024 * 1024),
    )(*between)


def solution(mesh):
    return jax.shard_map(
        body,
        mesh=mesh,
        in_specs=(
            P(None, "patch"),
            P("patch", None, None),
            P("patch", None, None),
            P("patch", None),
            P("patch", None, None, None, None),
            P(),
            P(None, None, "patch"),
            P("patch"),
            P("patch", None, None),
            P("patch", None, None, None),
            P("patch", None, None, None),
            P("patch", None),
        ),
        out_specs=(P(None, "patch"), P(None, None, "patch")),
        check_vma=False,
    )
```

time: 31.9 us -> 28 us (0.88)
  Pallas kernels: 31 us -> 27.2 us
    pallas_call x1, Pallas kernels: 28.2 us -> 24.9 us  [body(): pl.pallas_call(functools.partial(couple, size), name='couple', out_shape=...]
    pallas_call x1, Pallas kernels: 2.84 us -> 2.29 us  [body(): pl.pallas_call(scatter, name='scatter', out_shape=(jax.ShapeDtypeStruct((...]
where the time goes in v4:
time: 28 us; the launch traced here: 27.9 us
  Pallas kernels  27.2 us (97%)
  between operations  0.64 us (2%)
    pallas_call x1, Pallas kernels, body(): pl.pallas_call(functools.partial(couple, size), name='couple', out_shape=...  24.9 us
    pallas_call x1, Pallas kernels, body(): pl.pallas_call(scatter, name='scatter', out_shape=(jax.ShapeDtypeStruct((...  2.29 us

profile of v4, /device:TPU:0, one launch (start us, length us, event | category | flops | bytes accessed | tf_op | source)
XLA Modules:
  0.0 27.9 jit_solution(12000197472739267433)
XLA Ops:
  0.6 24.9 %couple.1 = (f32[32,2,128,128]{3,2,1,0:T(8,128)S(1)}, f32[8,4096]{1,0:T(8,128)S(1)}, bf16[256,256]{1,0:T(8,128)(2,1)S(1)}, bf16[256,128]{1,0:T(8,128)(2,1)S(1)},...) custom-call(s32[5,1,8]{2,1,0:T(1,128)} %bitcast.10, s32[5,1,8]{2,1,0:T(1,128)} %bitcast.11, s32[1,5]{1,0:T(1,128)} %cnt_h.1, ...), custom_call_target="tpu_custom_call" | custom-call | tf_op jit(solution)/shard_map/couple/pallas_call | solution.py:351
  25.6 2.3 %scatter.1 = (f32[8,4096]{1,0:T(8,128)}, f32[2,128,4096]{2,1,0:T(8,128)}) custom-call(f32[32,2,128,128]{3,2,1,0:T(8,128)S(1)} %get-tuple-element.8.x, f32[8,4096]{1,0:T(8,128)S(1)} %get-tuple-element.9.line, bf16[256,256]{1,0:T(8,128)(2,1)S(1)} %get-tuple-element.10.values_v, bf16[256,128]{1,0:T(8,128)(2,1)S(1)} %get-tuple-element.11.low_v, ...), custom_call_target="tpu_custom_call" | custom-call | tf_op jit(solution)/shard_map/scatter/pallas_call | solution.py:401

commit v5 on v4

--- a/solution.py
+++ b/solution.py
@@ -47,24 +47,39 @@
     send_h, tgt_h, cnt_h, coup_h, rows_h, atm_h, hs_h, hg_h, wet_h, tracer_h, mix_h, w_h,
     x, line, last_v, last_low, last_high, quarter_o,
     send_s, tgt_s, cnt_s, coup_s, rows_s, atm_v, hs_v, hg_v, wet_v,
-    m, w, blocks, outg, arr, contrib, ofs, surf, scale, sent, low_t, high_t, hout, v,
-    small, xsem, msem, wsem, fs, fr, hsend, hrecv,
+    m, w, blocks, outg, relay, arr, contrib, ofs, surf, scale, sent, low_t, high_t, hout, v,
+    small, xsem, msem, wsem, fs, fr, rs, rr, hsend, hrecv,
 ):
     me = lax.axis_index("patch")
 
     def at(offset):
         return lax.rem(me + (offset + size), size)
 
+    core = lax.rem(me, 2)
+    near = size - size // LINE
+    at_start = me < 2
+    at_end = me >= size - 2
+    at_relay = (me >= near) & (me < near + 2)
+
     barrier = pltpu.get_barrier_semaphore()
+
+    def hello(device):
+        pl.semaphore_signal(barrier, inc=1, device_id=(device,), device_id_type=MESH)
+
     for offset in HALO_OFFSETS:
-        pl.semaphore_signal(barrier, inc=1, device_id=(at(offset),), device_id_type=MESH)
+        if offset < 0:
+            hello(at(offset))
+        else:
+            pl.when(me + offset < size)(functools.partial(hello, at(offset)))
+    pl.when(at_end)(functools.partial(hello, near))
+    pl.when(me == size - 1)(functools.partial(hello, near + 1))
+    pl.when(at_start)(functools.partial(hello, near + core))
+    pl.when(at_relay)(functools.partial(hello, core))
 
     chip = lax.rem(me // 2, LINE)
     top = (chip + 1) // LINE
     foot = (LINE - chip) // LINE
     upper = chip // (LINE // 2)
-    core = lax.rem(me, 2)
-
     def choose(i):
         high, low = WAIT_ORDERS
         above = high[0][i] * (1 - core) + high[1][i] * core
@@ -155,17 +170,52 @@
             x[b, 0] = base[:, :BLK]
             x[b, 1] = base[:, BLK:]
 
-    pl.semaphore_wait(barrier, len(HALO_OFFSETS))
+    greeted = len(HALO_OFFSETS)
+    for who, amount in ((0, greeted - 1), (near, greeted + 3), (near + 1, greeted + 2)):
+        pl.when(me == who)(functools.partial(pl.semaphore_wait, barrier, amount))
+    pl.when((me != 0) & jnp.logical_not(at_relay))(
+        functools.partial(pl.semaphore_wait, barrier, greeted)
+    )
+
+    def flux_copy(d):
+        return pltpu.make_async_remote_copy(
+            src_ref=outg.at[d], dst_ref=arr.at[d], send_sem=fs.at[d], recv_sem=fr.at[d],
+            device_id=(at(FLUX_OFFSETS[d]),), device_id_type=MESH,
+        )
+
+    def to_relay(d):
+        return pltpu.make_async_remote_copy(
+            src_ref=outg.at[d], dst_ref=relay.at[d], send_sem=fs.at[d], recv_sem=rr.at[d],
+            device_id=(near + core,), device_id_type=MESH,
+        )
+
+    def from_relay(d, device):
+        return pltpu.make_async_remote_copy(
+            src_ref=relay.at[d], dst_ref=arr.at[d], send_sem=rs.at[d], recv_sem=fr.at[d],
+            device_id=(device,), device_id_type=MESH,
+        )
 
     flux = []
     for d in range(SPAN):
-        if FLUX_OFFSETS[d] != 0:
-            copy = pltpu.make_async_remote_copy(
-                src_ref=outg.at[d], dst_ref=arr.at[d], send_sem=fs.at[d], recv_sem=fr.at[d],
-                device_id=(at(FLUX_OFFSETS[d]),), device_id_type=MESH,
-            )
-            copy.start()
-            flux.append(copy)
+        offset = FLUX_OFFSETS[d]
+        if offset == 0:
+            continue
+        flux.append(flux_copy(d))
+        if offset > 0:
+            flux[-1].start()
+        else:
+            pl.when(me + offset >= 0)(flux[-1].start)
+            pl.when(me + offset < 0)(to_relay(d).start)
+
+    @pl.when(at_relay)
+    def _():
+        to_relay(0).wait_recv()
+        from_relay(0, size - 2 + core).start()
+
+    @pl.when(me == near)
+    def _():
+        to_relay(1).wait_recv()
+        from_relay(1, size - 1).start()
 
     for i in range(OBLK // PER):
         solve(i)
@@ -302,6 +352,8 @@
         last_v[t * LEV : (t + 1) * LEV] = v[last, t]
     for copy in flux:
         copy.wait_send()
+    pl.when(at_relay)(from_relay(0, size - 2 + core).wait_send)
+    pl.when(me == near)(from_relay(1, size - 1).wait_send)
     for h in order:
         for t in range(NTR):
             halo_copy(h, t).wait_send()
@@ -375,6 +427,7 @@
             pltpu.VMEM((SPAN, CAP, BLK, BLK), bf16),
             pltpu.VMEM((32 * F, BLK), f32),
             pltpu.VMEM((SPAN, CAP * F, BLK), bf16),
+            pltpu.VMEM((2, CAP * F, BLK), bf16),
             pltpu.VMEM((SPAN, CAP * F, BLK), bf16),
             pltpu.VMEM((48 * F, BLK), f32),
             pltpu.VMEM((OBLK * F, BLK), f32),
@@ -386,7 +439,7 @@
             pltpu.VMEM((HSPAN, NTR, LEV, picks), bf16),
             pltpu.VMEM((HSPAN, NTR, LEV, picks), bf16),
             dma((9,)), dma((OBLK // PER,)), dma((OBLK // PER,)), dma(()),
-            dma((SPAN,)), dma((SPAN,)), dma((HSPAN, NTR)), dma((HSPAN, NTR)),
+            dma((SPAN,)), dma((SPAN,)), dma((2,)), dma((2,)), dma((HSPAN, NTR)), dma((HSPAN, NTR)),
         ],
         compiler_params=pltpu.CompilerParams(
             collective_id=0, has_side_effects=True, vmem_limit_bytes=24 * 1024 * 1024

time: 28 us -> 26.2 us (0.936)
  Pallas kernels: 27.2 us -> 25.4 us
    pallas_call x1, Pallas kernels: 24.9 us -> 23.1 us  [body(): pl.pallas_call(functools.partial(couple, size), name='couple', out_shape=...]
where the time goes in v5:
time: 26.2 us; the launch traced here: 26.1 us
  Pallas kernels  25.4 us (97%)
  between operations  0.64 us (2%)
    pallas_call x1, Pallas kernels, body(): pl.pallas_call(functools.partial(couple, size), name='couple', out_shape=...  23.1 us
    pallas_call x1, Pallas kernels, body(): pl.pallas_call(scatter, name='scatter', out_shape=(jax.ShapeDtypeStruct((...  2.29 us

profile of v5, /device:TPU:0, one launch (start us, length us, event | category | flops | bytes accessed | tf_op | source)
XLA Modules:
  0.0 26.1 jit_solution(835324644099941689)
XLA Ops:
  0.6 23.1 %couple.1 = (f32[32,2,128,128]{3,2,1,0:T(8,128)S(1)}, f32[8,4096]{1,0:T(8,128)S(1)}, bf16[256,256]{1,0:T(8,128)(2,1)S(1)}, bf16[256,128]{1,0:T(8,128)(2,1)S(1)},...) custom-call(s32[5,1,8]{2,1,0:T(1,128)} %bitcast.10, s32[5,1,8]{2,1,0:T(1,128)} %bitcast.11, s32[1,5]{1,0:T(1,128)} %cnt_h.1, ...), custom_call_target="tpu_custom_call" | custom-call | tf_op jit(solution)/shard_map/couple/pallas_call | solution.py:403
  23.8 2.3 %scatter.1 = (f32[8,4096]{1,0:T(8,128)}, f32[2,128,4096]{2,1,0:T(8,128)}) custom-call(f32[32,2,128,128]{3,2,1,0:T(8,128)S(1)} %get-tuple-element.8.x, f32[8,4096]{1,0:T(8,128)S(1)} %get-tuple-element.9.line, bf16[256,256]{1,0:T(8,128)(2,1)S(1)} %get-tuple-element.10.values_v, bf16[256,128]{1,0:T(8,128)(2,1)S(1)} %get-tuple-element.11.low_v, ...), custom_call_target="tpu_custom_call" | custom-call | tf_op jit(solution)/shard_map/scatter/pallas_call | solution.py:454

commit v6 on v5

--- a/solution.py
+++ b/solution.py
@@ -55,11 +55,16 @@
     def at(offset):
         return lax.rem(me + (offset + size), size)
 
-    core = lax.rem(me, 2)
-    near = size - size // LINE
-    at_start = me < 2
-    at_end = me >= size - 2
-    at_relay = (me >= near) & (me < near + 2)
+    plane = size // LINE
+    near = 2 * LINE - 1
+    spot = lax.rem(me, plane)
+    level = me // plane
+    closing = (level + 1) // LINE
+    relay_spot = closing + near * (1 - closing)
+    mine = me - spot + relay_spot
+    opening = (LINE - level) // LINE
+    theirs = at(-plane) - spot + opening + near * (1 - opening)
+    at_relay = me == mine
 
     barrier = pltpu.get_barrier_semaphore()
 
@@ -70,16 +75,23 @@
         if offset < 0:
             hello(at(offset))
         else:
-            pl.when(me + offset < size)(functools.partial(hello, at(offset)))
-    pl.when(at_end)(functools.partial(hello, near))
-    pl.when(me == size - 1)(functools.partial(hello, near + 1))
-    pl.when(at_start)(functools.partial(hello, near + core))
-    pl.when(at_relay)(functools.partial(hello, core))
+            pl.when(spot + offset < plane)(functools.partial(hello, at(offset)))
+    pl.when(spot >= plane - 2)(functools.partial(hello, mine))
+    pl.when(spot < 2)(functools.partial(hello, theirs))
+    last_pair = me - spot + plane - 2
+    next_pair = lax.rem(me - spot + plane, size)
+
+    @pl.when(at_relay)
+    def _():
+        for c in range(2):
+            hello(next_pair + c)
 
     chip = lax.rem(me // 2, LINE)
     top = (chip + 1) // LINE
     foot = (LINE - chip) // LINE
     upper = chip // (LINE // 2)
+    core = lax.rem(me, 2)
+
     def choose(i):
         high, low = WAIT_ORDERS
         above = high[0][i] * (1 - core) + high[1][i] * core
@@ -171,9 +183,9 @@
             x[b, 1] = base[:, BLK:]
 
     greeted = len(HALO_OFFSETS)
-    for who, amount in ((0, greeted - 1), (near, greeted + 3), (near + 1, greeted + 2)):
-        pl.when(me == who)(functools.partial(pl.semaphore_wait, barrier, amount))
-    pl.when((me != 0) & jnp.logical_not(at_relay))(
+    pl.when(at_relay)(functools.partial(pl.semaphore_wait, barrier, 2 * greeted))
+    pl.when(spot == 0)(functools.partial(pl.semaphore_wait, barrier, greeted - 1))
+    pl.when((spot != 0) & jnp.logical_not(at_relay))(
         functools.partial(pl.semaphore_wait, barrier, greeted)
     )
 
@@ -183,16 +195,18 @@
             device_id=(at(FLUX_OFFSETS[d]),), device_id_type=MESH,
         )
 
-    def to_relay(d):
+    def to_relay(d, c):
+        slot = d + 2 * c
         return pltpu.make_async_remote_copy(
-            src_ref=outg.at[d], dst_ref=relay.at[d], send_sem=fs.at[d], recv_sem=rr.at[d],
-            device_id=(near + core,), device_id_type=MESH,
+            src_ref=outg.at[d], dst_ref=relay.at[slot], send_sem=fs.at[d], recv_sem=rr.at[slot],
+            device_id=(theirs,), device_id_type=MESH,
         )
 
-    def from_relay(d, device):
+    def from_relay(slot):
+        d, c = ((0, 0), (1, 1), (0, 1))[slot]
         return pltpu.make_async_remote_copy(
-            src_ref=relay.at[d], dst_ref=arr.at[d], send_sem=rs.at[d], recv_sem=fr.at[d],
-            device_id=(device,), device_id_type=MESH,
+            src_ref=relay.at[slot], dst_ref=arr.at[d], send_sem=rs.at[slot], recv_sem=fr.at[d],
+            device_id=(last_pair + c,), device_id_type=MESH,
         )
 
     flux = []
@@ -204,18 +218,15 @@
         if offset > 0:
             flux[-1].start()
         else:
-            pl.when(me + offset >= 0)(flux[-1].start)
-            pl.when(me + offset < 0)(to_relay(d).start)
+            pl.when(spot + offset >= 0)(flux[-1].start)
+            for c in range(-offset):
+                pl.when(spot == c)(to_relay(d, c).start)
 
     @pl.when(at_relay)
     def _():
-        to_relay(0).wait_recv()
-        from_relay(0, size - 2 + core).start()
-
-    @pl.when(me == near)
-    def _():
-        to_relay(1).wait_recv()
-        from_relay(1, size - 1).start()
+        for slot, (d, c) in enumerate(((0, 0), (1, 0), (0, 1))):
+            to_relay(d, c).wait_recv()
+            from_relay(slot).start()
 
     for i in range(OBLK // PER):
         solve(i)
@@ -352,8 +363,12 @@
         last_v[t * LEV : (t + 1) * LEV] = v[last, t]
     for copy in flux:
         copy.wait_send()
-    pl.when(at_relay)(from_relay(0, size - 2 + core).wait_send)
-    pl.when(me == near)(from_relay(1, size - 1).wait_send)
+
+    @pl.when(at_relay)
+    def _():
+        for slot in range(3):
+            from_relay(slot).wait_send()
+
     for h in order:
         for t in range(NTR):
             halo_copy(h, t).wait_send()
@@ -427,7 +442,7 @@
             pltpu.VMEM((SPAN, CAP, BLK, BLK), bf16),
             pltpu.VMEM((32 * F, BLK), f32),
             pltpu.VMEM((SPAN, CAP * F, BLK), bf16),
-            pltpu.VMEM((2, CAP * F, BLK), bf16),
+            pltpu.VMEM((3, CAP * F, BLK), bf16),
             pltpu.VMEM((SPAN, CAP * F, BLK), bf16),
             pltpu.VMEM((48 * F, BLK), f32),
             pltpu.VMEM((OBLK * F, BLK), f32),
@@ -439,7 +454,7 @@
             pltpu.VMEM((HSPAN, NTR, LEV, picks), bf16),
             pltpu.VMEM((HSPAN, NTR, LEV, picks), bf16),
             dma((9,)), dma((OBLK // PER,)), dma((OBLK // PER,)), dma(()),
-            dma((SPAN,)), dma((SPAN,)), dma((2,)), dma((2,)), dma((HSPAN, NTR)), dma((HSPAN, NTR)),
+            dma((SPAN,)), dma((SPAN,)), dma((3,)), dma((3,)), dma((HSPAN, NTR)), dma((HSPAN, NTR)),
         ],
         compiler_params=pltpu.CompilerParams(
             collective_id=0, has_side_effects=True, vmem_limit_bytes=24 * 1024 * 1024

time: 26.2 us -> 25.4 us (0.969)
  Pallas kernels: 25.4 us -> 24.6 us
    pallas_call x1, Pallas kernels: 23.1 us -> 22.3 us  [body(): pl.pallas_call(functools.partial(couple, size), name='couple', out_shape=...]
where the time goes in v6:
time: 25.4 us; the launch traced here: 25.3 us
  Pallas kernels  24.6 us (97%)
  between operations  0.64 us (3%)
    pallas_call x1, Pallas kernels, body(): pl.pallas_call(functools.partial(couple, size), name='couple', out_shape=...  22.3 us
    pallas_call x1, Pallas kernels, body(): pl.pallas_call(scatter, name='scatter', out_shape=(jax.ShapeDtypeStruct((...  2.29 us

profile of v6, /device:TPU:0, one launch (start us, length us, event | category | flops | bytes accessed | tf_op | source)
XLA Modules:
  0.0 25.3 jit_solution(17800431598514510621)
XLA Ops:
  0.6 22.3 %couple.1 = (f32[32,2,128,128]{3,2,1,0:T(8,128)S(1)}, f32[8,4096]{1,0:T(8,128)S(1)}, bf16[256,256]{1,0:T(8,128)(2,1)S(1)}, bf16[256,128]{1,0:T(8,128)(2,1)S(1)},...) custom-call(s32[5,1,8]{2,1,0:T(1,128)} %bitcast.10, s32[5,1,8]{2,1,0:T(1,128)} %bitcast.11, s32[1,5]{1,0:T(1,128)} %cnt_h.1, ...), custom_call_target="tpu_custom_call" | custom-call | tf_op jit(solution)/shard_map/couple/pallas_call | solution.py:418
  23.0 2.3 %scatter.1 = (f32[8,4096]{1,0:T(8,128)}, f32[2,128,4096]{2,1,0:T(8,128)}) custom-call(f32[32,2,128,128]{3,2,1,0:T(8,128)S(1)} %get-tuple-element.8.x, f32[8,4096]{1,0:T(8,128)S(1)} %get-tuple-element.9.line, bf16[256,256]{1,0:T(8,128)(2,1)S(1)} %get-tuple-element.10.values_v, bf16[256,128]{1,0:T(8,128)(2,1)S(1)} %get-tuple-element.11.low_v, ...), custom_call_target="tpu_custom_call" | custom-call | tf_op jit(solution)/shard_map/scatter/pallas_call | solution.py:469

commit v7 on v6

--- a/solution.py
+++ b/solution.py
@@ -59,12 +59,13 @@
     near = 2 * LINE - 1
     spot = lax.rem(me, plane)
     level = me // plane
-    closing = (level + 1) // LINE
-    relay_spot = closing + near * (1 - closing)
-    mine = me - spot + relay_spot
     opening = (LINE - level) // LINE
+    mine = me - spot + near
     theirs = at(-plane) - spot + opening + near * (1 - opening)
-    at_relay = me == mine
+    at_relay = spot == near
+    at_stage = me == size - plane + 1
+    last_pair = me - spot + plane - 2
+    next_pair = lax.rem(me - spot + plane, size)
 
     barrier = pltpu.get_barrier_semaphore()
 
@@ -78,10 +79,9 @@
             pl.when(spot + offset < plane)(functools.partial(hello, at(offset)))
     pl.when(spot >= plane - 2)(functools.partial(hello, mine))
     pl.when(spot < 2)(functools.partial(hello, theirs))
-    last_pair = me - spot + plane - 2
-    next_pair = lax.rem(me - spot + plane, size)
-
-    @pl.when(at_relay)
+    pl.when(me == size - plane + near)(functools.partial(hello, size - plane + 1))
+
+    @pl.when(at_stage | (at_relay & (level < LINE - 1)))
     def _():
         for c in range(2):
             hello(next_pair + c)
@@ -183,11 +183,15 @@
             x[b, 1] = base[:, BLK:]
 
     greeted = len(HALO_OFFSETS)
-    pl.when(at_relay)(functools.partial(pl.semaphore_wait, barrier, 2 * greeted))
-    pl.when(spot == 0)(functools.partial(pl.semaphore_wait, barrier, greeted - 1))
-    pl.when((spot != 0) & jnp.logical_not(at_relay))(
-        functools.partial(pl.semaphore_wait, barrier, greeted)
-    )
+    closing = level == LINE - 1
+    for who, amount in (
+        (at_relay & jnp.logical_not(closing), 2 * greeted),
+        (at_relay & closing, greeted + 2),
+        (at_stage, greeted + 3),
+        (spot == 0, greeted - 1),
+        ((spot != 0) & jnp.logical_not(at_relay) & jnp.logical_not(at_stage), greeted),
+    ):
+        pl.when(who)(functools.partial(pl.semaphore_wait, barrier, amount))
 
     def flux_copy(d):
         return pltpu.make_async_remote_copy(
@@ -207,6 +211,13 @@
         return pltpu.make_async_remote_copy(
             src_ref=relay.at[slot], dst_ref=arr.at[d], send_sem=rs.at[slot], recv_sem=fr.at[d],
             device_id=(last_pair + c,), device_id_type=MESH,
+        )
+
+    def from_stage(slot):
+        return pltpu.make_async_remote_copy(
+            src_ref=relay.at[slot], dst_ref=relay.at[slot],
+            send_sem=rs.at[slot], recv_sem=rr.at[slot],
+            device_id=(mine,), device_id_type=MESH,
         )
 
     flux = []
@@ -227,6 +238,12 @@
         for slot, (d, c) in enumerate(((0, 0), (1, 0), (0, 1))):
             to_relay(d, c).wait_recv()
             from_relay(slot).start()
+
+    @pl.when(at_stage)
+    def _():
+        for slot, (d, c) in enumerate(((0, 0), (1, 0), (0, 1))):
+            to_relay(d, c).wait_recv()
+            from_stage(slot).start()
 
     for i in range(OBLK // PER):
         solve(i)
@@ -368,6 +385,11 @@
     def _():
         for slot in range(3):
             from_relay(slot).wait_send()
+
+    @pl.when(at_stage)
+    def _():
+        for slot in range(3):
+            from_stage(slot).wait_send()
 
     for h in order:
         for t in range(NTR):

time: 25.4 us -> 24.9 us (0.980)
  Pallas kernels: 24.6 us -> 24.1 us
    pallas_call x1, Pallas kernels: 22.3 us -> 21.8 us  [body(): pl.pallas_call(functools.partial(couple, size), name='couple', out_shape=...]
where the time goes in v7:
time: 24.9 us; the launch traced here: 24.8 us
  Pallas kernels  24.1 us (97%)
  between operations  0.64 us (3%)
    pallas_call x1, Pallas kernels, body(): pl.pallas_call(functools.partial(couple, size), name='couple', out_shape=...  21.8 us
    pallas_call x1, Pallas kernels, body(): pl.pallas_call(scatter, name='scatter', out_shape=(jax.ShapeDtypeStruct((...  2.29 us

profile of v7, /device:TPU:0, one launch (start us, length us, event | category | flops | bytes accessed | tf_op | source)
XLA Modules:
  0.0 24.8 jit_solution(1801986098597446501)
XLA Ops:
  0.6 21.8 %couple.1 = (f32[32,2,128,128]{3,2,1,0:T(8,128)S(1)}, f32[8,4096]{1,0:T(8,128)S(1)}, bf16[256,256]{1,0:T(8,128)(2,1)S(1)}, bf16[256,128]{1,0:T(8,128)(2,1)S(1)},...) custom-call(s32[5,1,8]{2,1,0:T(1,128)} %bitcast.10, s32[5,1,8]{2,1,0:T(1,128)} %bitcast.11, s32[1,5]{1,0:T(1,128)} %cnt_h.1, ...), custom_call_target="tpu_custom_call" | custom-call | tf_op jit(solution)/shard_map/couple/pallas_call | solution.py:440
  22.5 2.3 %scatter.1 = (f32[8,4096]{1,0:T(8,128)}, f32[2,128,4096]{2,1,0:T(8,128)}) custom-call(f32[32,2,128,128]{3,2,1,0:T(8,128)S(1)} %get-tuple-element.8.x, f32[8,4096]{1,0:T(8,128)S(1)} %get-tuple-element.9.line, bf16[256,256]{1,0:T(8,128)(2,1)S(1)} %get-tuple-element.10.values_v, bf16[256,128]{1,0:T(8,128)(2,1)S(1)} %get-tuple-element.11.low_v, ...), custom_call_target="tpu_custom_call" | custom-call | tf_op jit(solution)/shard_map/scatter/pallas_call | solution.py:491

commit v8 on v7

--- a/solution.py
+++ b/solution.py
@@ -34,14 +34,6 @@
     return hi, lo
 
 
-def split3(v):
-    hi, rest = v.astype(bf16), None
-    rest = v - hi.astype(f32)
-    mid = rest.astype(bf16)
-    low = (rest - mid.astype(f32)).astype(bf16)
-    return hi, mid, low
-
-
 def couple(
     size,
     send_h, tgt_h, cnt_h, coup_h, rows_h, atm_h, hs_h, hg_h, wet_h, tracer_h, mix_h, w_h,
@@ -269,15 +261,16 @@
     scale[...] = 1.0 - quarter * count
 
     lane = lax.broadcasted_iota(jnp.int32, (OBLK, BLK), 1)
+    seat = lane & 63
     target = jnp.full((OBLK, BLK), -1, jnp.int32)
     used = jnp.zeros((OBLK, BLK), jnp.int32)
     for d in range(SPAN):
-        used = jnp.where(lane // CAP == d, cnt_s[0, d], used)
+        used = jnp.where(seat // CAP == d, cnt_s[0, d], used)
         for c in range(CAP):
-            target = jnp.where(lane == d * CAP + c, tgt_s[d, 0, c], target)
+            target = jnp.where(seat == d * CAP + c, tgt_s[d, 0, c], target)
     here = (target == block32) & (lane % CAP < used)
-    place = jnp.where(here, 1.0, 0.0).astype(bf16)[:, :48]
-    contrib[320:384, :] = jnp.zeros((64, BLK), f32)
+    place = jnp.where(here, 1.0, 0.0).astype(bf16)
+    contrib[320:512, :] = jnp.zeros((192, BLK), f32)
 
     wcopy.wait()
     slot = lax.broadcasted_iota(jnp.int32, (32, BLK), 0) // F
@@ -309,13 +302,11 @@
     acc = [jnp.zeros((OBLK, BLK), f32) for _ in range(NTR)]
     for k in range(F // 2):
         pair = jnp.concatenate(
-            [contrib[pl.ds(2 * k, 48, stride=F), :], contrib[pl.ds(2 * k + 1, 48, stride=F), :]],
+            [contrib[pl.ds(2 * k, 64, stride=F), :], contrib[pl.ds(2 * k + 1, 64, stride=F), :]],
             axis=1,
         )
-        c1, c2, c3 = split3(pair)
-        total = jnp.dot(place, c1, preferred_element_type=f32)
-        total = total + jnp.dot(place, c2, preferred_element_type=f32)
-        total = total + jnp.dot(place, c3, preferred_element_type=f32)
+        halves = jnp.concatenate(split2(pair), axis=0)
+        total = jnp.dot(place, halves, preferred_element_type=f32)
         for q in range(2):
             f = 2 * k + q
             flux_f = total[:, q * BLK : (q + 1) * BLK] * wetf
@@ -346,20 +337,25 @@
                 tables, tiles = [], []
                 for b in (2 * k, 2 * k + 1):
                     tables.append(jnp.where(high == jnp.array(b, bf16), low, jnp.zeros_like(low)))
+                    if n < 3:
+                        first = jnp.broadcast_to(m[b, :, 0:1], (LEV, BLK))
                     if n == 0:
-                        first = jnp.broadcast_to(m[b, :, 0:1], (LEV, BLK))
                         for t in part:
                             mixed = x[b, t] + first * surf[t, b : b + 1, :]
-                            x[b, t] = mixed * scale[b : b + 1, :]
                             tiles.append(mixed.astype(bf16))
+                    elif n < 3:
+                        t = n - 1
+                        mixed = x[b, t] + first * surf[t, b : b + 1, :]
+                        x[b, t] = mixed * scale[b : b + 1, :]
                 if n == 0:
                     tile = jnp.concatenate(tiles, axis=1)
                     sent[k, rows] = tile
                 else:
                     tile = sent[k, rows]
-                picked = picked + jnp.dot(
+                found = jnp.dot(
                     tile, jnp.concatenate(tables, axis=0), preferred_element_type=f32
                 )
+                picked = jnp.where((row >> 8) == k, found, picked)
             for j, t in enumerate(part):
                 hout[h, t] = picked[j * LEV : (j + 1) * LEV].astype(bf16)
                 halo_copy(h, t).start()
@@ -466,7 +462,7 @@
             pltpu.VMEM((SPAN, CAP * F, BLK), bf16),
             pltpu.VMEM((3, CAP * F, BLK), bf16),
             pltpu.VMEM((SPAN, CAP * F, BLK), bf16),
-            pltpu.VMEM((48 * F, BLK), f32),
+            pltpu.VMEM((64 * F, BLK), f32),
             pltpu.VMEM((OBLK * F, BLK), f32),
             pltpu.VMEM((NTR, OBLK, BLK), f32),
             pltpu.VMEM((OBLK, BLK), f32),

time: 24.9 us -> 24.7 us (level)
  no operation moved by 1% of the time
where the time goes in v8:
time: 24.7 us; the launch traced here: 24.6 us
  Pallas kernels  23.9 us (97%)
  between operations  0.64 us (3%)
    pallas_call x1, Pallas kernels, body(): pl.pallas_call(functools.partial(couple, size), name='couple', out_shape=...  21.6 us
    pallas_call x1, Pallas kernels, body(): pl.pallas_call(scatter, name='scatter', out_shape=(jax.ShapeDtypeStruct((...  2.29 us

profile of v8, /device:TPU:0, one launch (start us, length us, event | category | flops | bytes accessed | tf_op | source)
XLA Modules:
  0.0 24.6 jit_solution(11188783091667786081)
XLA Ops:
  0.6 21.6 %couple.1 = (f32[32,2,128,128]{3,2,1,0:T(8,128)S(1)}, f32[8,4096]{1,0:T(8,128)S(1)}, bf16[256,256]{1,0:T(8,128)(2,1)S(1)}, bf16[256,128]{1,0:T(8,128)(2,1)S(1)},...) custom-call(s32[5,1,8]{2,1,0:T(1,128)} %bitcast.10, s32[5,1,8]{2,1,0:T(1,128)} %bitcast.11, s32[1,5]{1,0:T(1,128)} %cnt_h.1, ...), custom_call_target="tpu_custom_call" | custom-call | tf_op jit(solution)/shard_map/couple/pallas_call | solution.py:436
  22.3 2.3 %scatter.1 = (f32[8,4096]{1,0:T(8,128)}, f32[2,128,4096]{2,1,0:T(8,128)}) custom-call(f32[32,2,128,128]{3,2,1,0:T(8,128)S(1)} %get-tuple-element.8.x, f32[8,4096]{1,0:T(8,128)S(1)} %get-tuple-element.9.line, bf16[256,256]{1,0:T(8,128)(2,1)S(1)} %get-tuple-element.10.values_v, bf16[256,128]{1,0:T(8,128)(2,1)S(1)} %get-tuple-element.11.low_v, ...), custom_call_target="tpu_custom_call" | custom-call | tf_op jit(solution)/shard_map/scatter/pallas_call | solution.py:487

commit v9 on v8

--- a/solution.py
+++ b/solution.py
@@ -318,11 +318,12 @@
 
     sub = lax.broadcasted_iota(jnp.int32, (BLK, 2 * BLK), 0)
 
-    def halo_copy(h, t):
+    def halo_copy(h, t=None):
         offset = h - 2 + h // 2
         return pltpu.make_async_remote_copy(
-            src_ref=hout.at[h, t], dst_ref=v.at[h, t],
-            send_sem=hsend.at[h, t], recv_sem=hrecv.at[h, t],
+            src_ref=hout.at[h] if t is None else hout.at[h, t],
+            dst_ref=v.at[h] if t is None else v.at[h, t],
+            send_sem=hsend.at[h], recv_sem=hrecv.at[h],
             device_id=(at(offset),), device_id_type=MESH,
         )
 
@@ -358,7 +359,7 @@
                 picked = jnp.where((row >> 8) == k, found, picked)
             for j, t in enumerate(part):
                 hout[h, t] = picked[j * LEV : (j + 1) * LEV].astype(bf16)
-                halo_copy(h, t).start()
+            halo_copy(h, part[0] if n == 0 else None).start()
 
     for b in range(OBLK):
         line[:, b * BLK : (b + 1) * BLK] = ofs[b * F : (b + 1) * F, :]
@@ -367,12 +368,11 @@
     last_high[...] = high_t[last]
 
     for h in order[:-1]:
-        for t in range(NTR):
-            halo_copy(h, t).wait_recv()
+        halo_copy(h).wait_recv()
         values = jnp.concatenate([v[h, 0], v[h, 1]], axis=0)
         add_values(x, values, low_t[h], high_t[h], quarter_o)
+    halo_copy(last).wait_recv()
     for t in range(NTR):
-        halo_copy(last, t).wait_recv()
         last_v[t * LEV : (t + 1) * LEV] = v[last, t]
     for copy in flux:
         copy.wait_send()
@@ -388,8 +388,7 @@
             from_stage(slot).wait_send()
 
     for h in order:
-        for t in range(NTR):
-            halo_copy(h, t).wait_send()
+        halo_copy(h).wait_send()
 
 
 def add_values(x, values, low, high, quarter_v, out=None, ready=None):
@@ -472,7 +471,7 @@
             pltpu.VMEM((HSPAN, NTR, LEV, picks), bf16),
             pltpu.VMEM((HSPAN, NTR, LEV, picks), bf16),
             dma((9,)), dma((OBLK // PER,)), dma((OBLK // PER,)), dma(()),
-            dma((SPAN,)), dma((SPAN,)), dma((3,)), dma((3,)), dma((HSPAN, NTR)), dma((HSPAN, NTR)),
+            dma((SPAN,)), dma((SPAN,)), dma((3,)), dma((3,)), dma((HSPAN,)), dma((HSPAN,)),
         ],
         compiler_params=pltpu.CompilerParams(
             collective_id=0, has_side_effects=True, vmem_limit_bytes=24 * 1024 * 1024

time: 24.7 us -> 24.7 us (level)
  no operation moved by 1% of the time
where the time goes in v9:
time: 24.7 us; the launch traced here: 24.5 us
  Pallas kernels  23.9 us (97%)
  between operations  0.64 us (3%)
    pallas_call x1, Pallas kernels, body(): pl.pallas_call(functools.partial(couple, size), name='couple', out_shape=...  21.6 us
    pallas_call x1, Pallas kernels, body(): pl.pallas_call(scatter, name='scatter', out_shape=(jax.ShapeDtypeStruct((...  2.29 us

profile of v9, /device:TPU:0, one launch (start us, length us, event | category | flops | bytes accessed | tf_op | source)
XLA Modules:
  0.0 24.5 jit_solution(9160378756445628804)
XLA Ops:
  0.6 21.6 %couple.1 = (f32[32,2,128,128]{3,2,1,0:T(8,128)S(1)}, f32[8,4096]{1,0:T(8,128)S(1)}, bf16[256,256]{1,0:T(8,128)(2,1)S(1)}, bf16[256,128]{1,0:T(8,128)(2,1)S(1)},...) custom-call(s32[5,1,8]{2,1,0:T(1,128)} %bitcast.10, s32[5,1,8]{2,1,0:T(1,128)} %bitcast.11, s32[1,5]{1,0:T(1,128)} %cnt_h.1, ...), custom_call_target="tpu_custom_call" | custom-call | tf_op jit(solution)/shard_map/couple/pallas_call | solution.py:435
  22.2 2.3 %scatter.1 = (f32[8,4096]{1,0:T(8,128)}, f32[2,128,4096]{2,1,0:T(8,128)}) custom-call(f32[32,2,128,128]{3,2,1,0:T(8,128)S(1)} %get-tuple-element.8.x, f32[8,4096]{1,0:T(8,128)S(1)} %get-tuple-element.9.line, bf16[256,256]{1,0:T(8,128)(2,1)S(1)} %get-tuple-element.10.values_v, bf16[256,128]{1,0:T(8,128)(2,1)S(1)} %get-tuple-element.11.low_v, ...), custom_call_target="tpu_custom_call" | custom-call | tf_op jit(solution)/shard_map/scatter/pallas_call | solution.py:486

commit v10 on v9

--- a/solution.py
+++ b/solution.py
@@ -212,6 +212,16 @@
             device_id=(mine,), device_id_type=MESH,
         )
 
+    both = pl.ds(0, 2)
+    to_relay_both = pltpu.make_async_remote_copy(
+        src_ref=outg.at[both], dst_ref=relay.at[both], send_sem=fs.at[0], recv_sem=rr.at[0],
+        device_id=(theirs,), device_id_type=MESH,
+    )
+    from_stage_both = pltpu.make_async_remote_copy(
+        src_ref=relay.at[both], dst_ref=relay.at[both], send_sem=rs.at[0], recv_sem=rr.at[0],
+        device_id=(mine,), device_id_type=MESH,
+    )
+
     flux = []
     for d in range(SPAN):
         offset = FLUX_OFFSETS[d]
@@ -222,20 +232,24 @@
             flux[-1].start()
         else:
             pl.when(spot + offset >= 0)(flux[-1].start)
-            for c in range(-offset):
-                pl.when(spot == c)(to_relay(d, c).start)
+            if d == 0:
+                pl.when(spot == 0)(to_relay_both.start)
+                pl.when(spot == 1)(to_relay(0, 1).start)
 
     @pl.when(at_relay)
     def _():
-        for slot, (d, c) in enumerate(((0, 0), (1, 0), (0, 1))):
-            to_relay(d, c).wait_recv()
-            from_relay(slot).start()
+        to_relay_both.wait_recv()
+        from_relay(0).start()
+        from_relay(1).start()
+        to_relay(0, 1).wait_recv()
+        from_relay(2).start()
 
     @pl.when(at_stage)
     def _():
-        for slot, (d, c) in enumerate(((0, 0), (1, 0), (0, 1))):
-            to_relay(d, c).wait_recv()
-            from_stage(slot).start()
+        to_relay_both.wait_recv()
+        from_stage_both.start()
+        to_relay(0, 1).wait_recv()
+        from_stage(2).start()
 
     for i in range(OBLK // PER):
         solve(i)
@@ -374,7 +388,10 @@
     halo_copy(last).wait_recv()
     for t in range(NTR):
         last_v[t * LEV : (t + 1) * LEV] = v[last, t]
-    for copy in flux:
+    pl.when(spot == 0)(to_relay_both.wait_send)
+    for copy in flux[:2]:
+        pl.when(spot != 0)(copy.wait_send)
+    for copy in flux[2:]:
         copy.wait_send()
 
     @pl.when(at_relay)
@@ -384,8 +401,8 @@
 
     @pl.when(at_stage)
     def _():
-        for slot in range(3):
-            from_stage(slot).wait_send()
+        from_stage_both.wait_send()
+        from_stage(2).wait_send()
 
     for h in order:
         halo_copy(h).wait_send()

time: 24.7 us -> 24.9 us (level)
  no operation moved by 1% of the time
where the time goes in v10:
time: 24.9 us; the launch traced here: 24.7 us
  Pallas kernels  24.1 us (97%)
  between operations  0.64 us (3%)
    pallas_call x1, Pallas kernels, body(): pl.pallas_call(functools.partial(couple, size), name='couple', out_shape=...  21.8 us
    pallas_call x1, Pallas kernels, body(): pl.pallas_call(scatter, name='scatter', out_shape=(jax.ShapeDtypeStruct((...  2.29 us

profile of v10, /device:TPU:0, one launch (start us, length us, event | category | flops | bytes accessed | tf_op | source)
XLA Modules:
  0.0 24.7 jit_solution(16145491589290165188)
XLA Ops:
  0.6 21.8 %couple.1 = (f32[32,2,128,128]{3,2,1,0:T(8,128)S(1)}, f32[8,4096]{1,0:T(8,128)S(1)}, bf16[256,256]{1,0:T(8,128)(2,1)S(1)}, bf16[256,128]{1,0:T(8,128)(2,1)S(1)},...) custom-call(s32[5,1,8]{2,1,0:T(1,128)} %bitcast.10, s32[5,1,8]{2,1,0:T(1,128)} %bitcast.11, s32[1,5]{1,0:T(1,128)} %cnt_h.1, ...), custom_call_target="tpu_custom_call" | custom-call | tf_op jit(solution)/shard_map/couple/pallas_call | solution.py:452
  22.4 2.3 %scatter.1 = (f32[8,4096]{1,0:T(8,128)}, f32[2,128,4096]{2,1,0:T(8,128)}) custom-call(f32[32,2,128,128]{3,2,1,0:T(8,128)S(1)} %get-tuple-element.8.x, f32[8,4096]{1,0:T(8,128)S(1)} %get-tuple-element.9.line, bf16[256,256]{1,0:T(8,128)(2,1)S(1)} %get-tuple-element.10.values_v, bf16[256,128]{1,0:T(8,128)(2,1)S(1)} %get-tuple-element.11.low_v, ...), custom_call_target="tpu_custom_call" | custom-call | tf_op jit(solution)/shard_map/scatter/pallas_call | solution.py:503
